TPU v7x, 32 devices: a whole 2x2x4 slice. The times are simulated.
32 devices in a mesh: yz: 8 (over z, y), x: 4 (over x, core).
Axes of the slice: x: 2, y: 2, z: 4, core: 2. Of those that a mesh axis runs over, the one named last changes fastest.
Arguments:
- h: bfloat16 [64, 4096], P(None, ('x', 'yz'))
- g: bfloat16 [2, 4096], P(None, ('x', 'yz'))
- wq: bfloat16 [2, 4096, 4096], P(None, 'x', 'yz')
- wk: bfloat16 [2, 4096, 4096], P(None, 'x', 'yz')
- wv: bfloat16 [2, 4096, 4096], P(None, 'x', 'yz')
- w_in: bfloat16 [2, 4096, 16384], P(None, 'x', 'yz')
- wo: bfloat16 [2, 4096, 4096], P(None, 'yz', 'x')
- w_out: bfloat16 [2, 16384, 4096], P(None, 'yz', 'x')
- k_cache: bfloat16 [2, 64, 32, 256, 128], P(None, None, ('yz', 'x'))
- v_cache: bfloat16 [2, 64, 32, 256, 128], P(None, None, ('yz', 'x'))
- lens: int32 [64], replicated
Outputs:
- output 1: bfloat16 [64, 4096], P(None, ('x', 'yz'))
- output 2: bfloat16 [2, 64, 32, 128], P(None, None, ('yz', 'x'))
- output 3: bfloat16 [2, 64, 32, 128], P(None, None, ('yz', 'x'))
All inputs are finite; a program needn't handle non-finite values.
Results may differ from a plain program's by a relative error of at most 0.02.
Values are sent between devices in bfloat16 or wider.
A program may use at most 1 GiB of HBM per device.

v0:
```python
import jax
import jax.numpy as jnp
from jax import lax
from jax.sharding import PartitionSpec as P

EPS = 1e-6


def _rope(t, lens):
    half = t.shape[-1] // 2
    inv = 10000.0 ** (-jnp.arange(half, dtype=jnp.float32) / half)
    ang = lens.astype(jnp.float32)[:, None, None] * inv
    c, s = jnp.cos(ang), jnp.sin(ang)
    tf = t.astype(jnp.float32)
    a, b = tf[..., :half], tf[..., half:]
    return jnp.concatenate([a * c - b * s, b * c + a * s], axis=-1).astype(jnp.bfloat16)


def _attend(q, kc, vc, k, v, lens):
    scale = q.shape[-1] ** -0.5
    s = jnp.einsum('bhd,bhsd->bhs', q, kc, preferred_element_type=jnp.float32) * scale
    pos = jnp.arange(kc.shape[2])
    s = jnp.where(pos[None, None, :] < lens[:, None, None], s, -jnp.inf)
    sn = jnp.einsum('bhd,bhd->bh', q, k, preferred_element_type=jnp.float32) * scale
    m = jnp.maximum(jnp.max(s, axis=-1), sn)
    p = jnp.exp(s - m[..., None])
    pn = jnp.exp(sn - m)
    den = jnp.sum(p, axis=-1) + pn
    o = jnp.einsum('bhs,bhsd->bhd', p.astype(jnp.bfloat16), vc, preferred_element_type=jnp.float32)
    o = o + pn[..., None] * v.astype(jnp.float32)
    return (o / den[..., None]).astype(jnp.bfloat16)


def solution(mesh):
    X = mesh.shape['x']
    Y = mesh.shape['yz']
    act = P(None, ('x', 'yz'))
    w_first = P(None, 'x', 'yz')
    w_second = P(None, 'yz', 'x')
    cache = P(None, None, ('yz', 'x'), None, None)
    new = P(None, None, ('yz', 'x'), None)

    def body(h, g, wq, wk, wv, w_in, wo, w_out, kc, vc, lens):
        bsz = h.shape[0]
        hl, dh = kc.shape[2], kc.shape[4]
        hdn = hl * dh
        e_total = h.shape[1] * X * Y
        ks, vs = [], []
        for l in range(wq.shape[0]):
            hf = h.astype(jnp.float32)
            ss = lax.psum(jnp.sum(hf * hf, axis=-1, keepdims=True), ('yz', 'x'))
            x = (hf * lax.rsqrt(ss / e_total + EPS) * g[l].astype(jnp.float32)).astype(jnp.bfloat16)
            xg = lax.all_gather(x, 'yz', axis=1, tiled=True)
            parts = [jnp.dot(xg, w[l], preferred_element_type=jnp.float32).astype(jnp.bfloat16).reshape(bsz, X, -1)
                     for w in (wq, wk, wv, w_in)]
            r = lax.psum_scatter(jnp.concatenate(parts, axis=2), 'x', scatter_dimension=1, tiled=True)[:, 0]
            q = _rope(r[:, :hdn].reshape(bsz, hl, dh), lens)
            k = _rope(r[:, hdn:2 * hdn].reshape(bsz, hl, dh), lens)
            v = r[:, 2 * hdn:3 * hdn].reshape(bsz, hl, dh)
            f = jax.nn.gelu(r[:, 3 * hdn:].astype(jnp.float32), approximate=True).astype(jnp.bfloat16)
            o = _attend(q, kc[l], vc[l], k, v, lens).reshape(bsz, hdn)
            ga = lax.all_gather(jnp.concatenate([o, f], axis=1), 'x', axis=1)
            og = ga[:, :, :hdn].reshape(bsz, -1)
            fg = ga[:, :, hdn:].reshape(bsz, -1)
            yp = (jnp.dot(og, wo[l], preferred_element_type=jnp.float32)
                  + jnp.dot(fg, w_out[l], preferred_element_type=jnp.float32)).astype(jnp.bfloat16)
            y = lax.psum_scatter(yp, 'yz', scatter_dimension=1, tiled=True)
            h = (hf + y.astype(jnp.float32)).astype(jnp.bfloat16)
            ks.append(k)
            vs.append(v)
        return h, jnp.stack(ks), jnp.stack(vs)

    return jax.shard_map(
        body, mesh=mesh,
        in_specs=(act, act, w_first, w_first, w_first, w_first, w_second, w_second, cache, cache, P(None)),
        out_specs=(act, new, new), check_vma=False)
```

profile of v0, /device:TPU:0, one launch (start us, length us, event | category | flops | bytes accessed | tf_op | source)
XLA Modules:
  0.0 386.0 jit_solution(4979503444880474409)
XLA Ops:
  7.2 0.0 reduce-scatter.9.cloned.1.call-start
  7.2 0.8 fusion.112
  8.0 42.0 %psum.14 = f32[64,1]{0,1:T(1,128)S(1)} all-reduce(f32[64,1]{0,1:T(1,128)S(1)} %bitcast.239), channel_id=1, replica_groups=mesh['yz'=8,'x'=4] {'yz','x'}, use_global_device_ids=true, to_apply=%region_1.0 | all-reduce | flops 64 | bytes 512 | tf_op jit(solution)/shard_map/psum | solution.py:51
  50.0 0.7 bitcast_convert_fusion.1
  50.8 0.8 fusion.114
  51.5 30.8 %all_gather.18 = bf16[64,1024]{1,0:T(8,128)(2,1)S(1)} all-gather(bf16[64,128]{1,0:T(8,128)(2,1)S(1)} %fusion.114), channel_id=1, replica_groups=mesh['yz'=8,'x'=4] {'yz'}, dimensions={1}, use_global_device_ids=true | all-gather | bytes 147456 | tf_op jit(solution)/shard_map/all_gather | solution.py:53
  82.3 1.5 fusion.34
  83.8 1.5 fusion.33
  85.4 1.5 fusion.32
  86.9 3.0 fusion.24
  90.0 0.8 pad_maximum_fusion
  90.9 0.0 reduce-scatter.13.cloned.1.call-start
  91.0 20.7 %reduce-scatter.9.cloned.1.call-done = bf16[64,1,896]{2,0,1:T(8,128)(2,1)} async-done(((bf16[64,4,896]{2,0,1:T(8,128)(2,1)}), bf16[64,1,896]{2,0,1:T(8,128)(2,1)}) %reduce-scatter.9.cloned.1.call-update) | async-done | bytes 114704 | tf_op jit(solution)/shard_map/reduce_scatter | solution.py:56
  111.7 0.9 fusion.59
  112.6 0.8 slice_bitcast_fusion.5
  113.4 0.2 fusion.101
  113.6 0.1 fusion.135
  113.7 3.4 fusion.12
  117.0 0.2 fusion.94
  117.2 0.2 fusion.123
  117.4 0.2 fusion.74
  117.6 2.8 fusion.10
  120.5 1.0 divide_convert_fusion.1
  121.5 6.0 %all-gather = bf16[64,2560]{1,0:T(8,128)(2,1)S(1)} all-gather(bf16[64,640]{1,0:T(8,128)(2,1)S(1)} %pad_maximum_fusion.2), channel_id=2, replica_groups=mesh['yz'=8,'x'=4] {'x'}, dimensions={1}, use_global_device_ids=true | all-gather | bytes 409600 | tf_op jit(solution)/shard_map/all_gather | solution.py:62
  127.4 0.1 reshape.397
  127.5 0.1 slice.161
  127.7 3.0 fusion.8
  130.8 0.3 fusion.30
  131.1 0.8 copy.54
  131.9 0.0 reduce-scatter.11.cloned.1.call-start
  132.0 62.7 %reduce-scatter.13.cloned.1.call-done = bf16[128,64]{1,0:T(8,128)(2,1)} async-done(((bf16[1024,64]{1,0:T(8,128)(2,1)}), bf16[128,64]{1,0:T(8,128)(2,1)}) %reduce-scatter.13.cloned.1.call-update) | async-done | bytes 16400
  194.6 0.8 copy.55
  195.5 0.1 fusion.116
  195.6 40.2 %psum.15 = f32[64,1]{0,1:T(1,128)S(1)} all-reduce(f32[64,1]{0,1:T(1,128)S(1)} %bitcast.238), channel_id=1, replica_groups=mesh['yz'=8,'x'=4] {'yz','x'}, use_global_device_ids=true, to_apply=%region_7.8 | all-reduce | flops 64 | bytes 512 | tf_op jit(solution)/shard_map/psum | solution.py:51
  235.8 0.1 fusion.118
  235.9 30.7 %all_gather.21 = bf16[64,1024]{1,0:T(8,128)(2,1)S(1)} all-gather(bf16[64,128]{1,0:T(8,128)(2,1)S(1)} %fusion.118), channel_id=1, replica_groups=mesh['yz'=8,'x'=4] {'yz'}, dimensions={1}, use_global_device_ids=true | all-gather | bytes 147456 | tf_op jit(solution)/shard_map/all_gather | solution.py:53
  266.5 1.5 fusion.37
  268.0 1.5 fusion.36
  269.6 1.5 fusion.35
  271.1 3.0 fusion.27
  274.2 0.8 pad_maximum_fusion.1
  275.1 0.0 reduce-scatter.15.cloned.1.call-start
  275.1 20.1 %reduce-scatter.11.cloned.1.call-done = bf16[64,1,896]{2,0,1:T(8,128)(2,1)} async-done(((bf16[64,4,896]{2,0,1:T(8,128)(2,1)}), bf16[64,1,896]{2,0,1:T(8,128)(2,1)}) %reduce-scatter.11.cloned.1.call-update) | async-done | bytes 114704 | tf_op jit(solution)/shard_map/reduce_scatter | solution.py:56
  295.2 0.9 fusion.65
  296.1 0.8 slice_bitcast_fusion.4
  296.9 0.2 fusion.109
  297.1 0.1 fusion.134
  297.2 3.4 fusion.4
  300.6 0.2 fusion.95
  300.7 0.2 fusion.122
  301.0 0.2 fusion.76
  301.2 2.8 fusion.2
  304.0 0.8 divide_convert_fusion
  304.8 6.0 %all-gather.1 = bf16[64,2560]{1,0:T(8,128)(2,1)S(1)} all-gather(bf16[64,640]{1,0:T(8,128)(2,1)S(1)} %pad_maximum_fusion.3), channel_id=3, replica_groups=mesh['yz'=8,'x'=4] {'x'}, dimensions={1}, use_global_device_ids=true | all-gather | bytes 409600 | tf_op jit(solution)/shard_map/all_gather | solution.py:62
  310.8 0.1 reshape.398
  310.9 0.1 slice.171
  311.1 3.0 fusion
  314.1 0.3 fusion.31
  314.4 0.8 copy.56
  315.3 0.6 pad_maximum_fusion.4
  315.9 0.7 maximum_maximum_fusion
  316.6 61.4 %reduce-scatter.15.cloned.1.call-done = bf16[128,64]{1,0:T(8,128)(2,1)} async-done(((bf16[1024,64]{1,0:T(8,128)(2,1)}), bf16[128,64]{1,0:T(8,128)(2,1)}) %reduce-scatter.15.cloned.1.call-update) | async-done | bytes 16400
  378.0 0.8 copy.57
  378.8 0.6 fusion.119
  (31 shorter events, 0.4 us)
Async XLA Ops:
  7.2 104.5 %reduce-scatter.9.cloned.1.call-start = ((), (), s32[]{:S(2)}) async-start(), calls=%async_computation.4 | async-start | bytes 573440 | tf_op jit(solution)/shard_map/reduce_scatter | solution.py:56
  85.4 5.6 %copy-start.2 = (s32[64]{0:T(128)S(1)}, s32[64]{0:T(128)}, u32[]{:S(2)}) copy-start(s32[64]{0:T(128)} %param.21) | copy-start | bytes 772
  90.9 103.7 %reduce-scatter.13.cloned.1.call-start = ((), (), s32[]{:S(2)}) async-start(), calls=%async_computation.6 | async-start | bytes 294912
  120.5 10.3 %copy-start = (bf16[2,512,1024]{2,1,0:T(8,128)(2,1)S(1)}, bf16[2,512,1024]{2,1,0:T(8,128)(2,1)}, u32[]{:S(2)}) copy-start(bf16[2,512,1024]{2,1,0:T(8,128)(2,1)} %param.17) | copy-start | bytes 6291460
  127.5 67.9 %copy-start.1 = (bf16[64,128]{1,0:T(8,128)(2,1)S(1)}, bf16[64,128]{1,0:T(8,128)(2,1)}, u32[]{:S(2)}) copy-start(bf16[64,128]{1,0:T(8,128)(2,1)} %param.11) | copy-start | bytes 49156
  131.9 163.3 %reduce-scatter.11.cloned.1.call-start = ((), (), s32[]{:S(2)}) async-start(), calls=%async_computation.5 | async-start | bytes 573440 | tf_op jit(solution)/shard_map/reduce_scatter | solution.py:56
  275.1 102.9 %reduce-scatter.15.cloned.1.call-start = ((), (), s32[]{:S(2)}) async-start(), calls=%async_computation.7 | async-start | bytes 294912
Sparse Core Ops, SparseCore 0:
  91.0 20.6 reduce-scatter.8
  132.0 62.5 reduce-scatter.12
  275.2 19.9 reduce-scatter.10
  315.4 62.5 reduce-scatter.14
where the time goes:
time: 387 us; the launch traced here: 386 us
  waiting for transfers between devices  165 us (43%)
  blocking collectives  155 us (40%)
  matrix products  34.3 us (9%)
  between operations  14.1 us (4%)
  other arithmetic  13 us (3%)
  local copies, waits for them, and re-layouts  3.95 us (1%)
    unnamed x6, waiting for transfers between devices  124 us
    psum x2, blocking collectives, body(): ss = lax.psum(jnp.sum(hf * hf, axis=-1, keepdims=True), ('yz', 'x'))  82.1 us
    all_gather x2, blocking collectives, body(): xg = lax.all_gather(x, 'yz', axis=1, tiled=True)  61.4 us
    reduce_scatter x2, waiting for transfers between devices, body(): lax.psum_scatter(jnp.concatenate(parts, axis=2), 'x', scatter_dimension=1...  40.8 us
    dot_general x8, matrix products, body(): jnp.dot(xg, w[l], preferred_element_type=jnp.float32).astype(jnp.bfloat16)  15.2 us
    all_gather x2, blocking collectives, body(): ga = lax.all_gather(jnp.concatenate([o, f], axis=1), 'x', axis=1)  11.9 us
  transfers between devices with their start and end apart: 4, of which 4 were waited for; matrix products, arithmetic and copies ran while one was open for 0% of the time, Pallas kernels for 0%

commit v1 on v0

v1 whole, which is shorter than its diff:
```python
import functools
import math

import numpy as np

import jax
import jax.numpy as jnp
from jax import lax
from jax.experimental import pallas as pl
from jax.experimental.pallas import tpu as pltpu
from jax.sharding import PartitionSpec as P

EPS = 1e-6
MESH = pl.DeviceIdType.MESH
F32 = jnp.float32
BF16 = jnp.bfloat16


def _gelu(x):
    return 0.5 * x * (1.0 + jnp.tanh(math.sqrt(2.0 / math.pi) * (x + 0.044715 * (x * x * x))))


def _kernel(X, Y, e_total, h_ref, g_ref, lens_ref, inv_ref, wq, wk, wv, w_in, wo, w_out, kc, vc,
            h_out, k_out, v_out,
            wqkv_b, win_b, wo_b, wout_b, k_b, v_b,
            hcur, hbuf, gbuf, ssown, ssbuf, xs, cos_b, sin_b, lenb,
            pq, pf, rq, rf, q_b, sc_b, of32, obuf, fbuf, ybuf, ry,
            wsem, bsend, hrecv, grecv, ssend, srecv, psend, precv, asend, arecv, ysend, yrecv):
    me_y = lax.axis_index("yz")
    me_x = lax.axis_index("x")
    me = me_y * X + me_x
    N = X * Y
    L = wqkv_b.shape[0]
    B, BLK = h_ref.shape
    S, D = kc.shape[2], kc.shape[3]
    E = wq.shape[1]
    HD = wq.shape[2]
    FL = w_in.shape[2]
    FB = FL // X
    half = D // 2

    def load(l):
        out = []
        for i, w in enumerate((wq, wk, wv)):
            out.append(pltpu.make_async_copy(w.at[l], wqkv_b.at[l, :, pl.ds(i * HD, HD)], wsem.at[l, 0]))
        ce = E // 4
        for i in range(4):
            rows = pl.ds(i * ce, ce)
            out.append(pltpu.make_async_copy(w_in.at[l, rows], win_b.at[l, rows], wsem.at[l, 1]))
        cb = B // 4
        for i in range(4):
            rows = pl.ds(i * cb, cb)
            out.append(pltpu.make_async_copy(kc.at[l, rows], k_b.at[l, rows], wsem.at[l, 2]))
        for i in range(4):
            rows = pl.ds(i * cb, cb)
            out.append(pltpu.make_async_copy(vc.at[l, rows], v_b.at[l, rows], wsem.at[l, 3]))
        cf = FL // 4
        for i in range(4):
            rows = pl.ds(i * cf, cf)
            out.append(pltpu.make_async_copy(w_out.at[l, rows], wout_b.at[l, rows], wsem.at[l, 4]))
        out.append(pltpu.make_async_copy(wo.at[l], wo_b.at[l], wsem.at[l, 5]))
        return out

    def wait_bytes(ref, sem):
        pltpu.make_async_copy(ref, ref, sem).wait()

    for l in range(L):
        for c in load(l):
            c.start()

    barrier = pltpu.get_barrier_semaphore()

    def greet(d, carry):
        t = lax.rem(me + d, N)
        pl.semaphore_signal(barrier, inc=1, device_id=(lax.div(t, X), lax.rem(t, X)), device_id_type=MESH)
        return carry

    lax.fori_loop(1, N, greet, 0)

    hcur[...] = h_ref[...]
    gbuf[me_y] = g_ref[...]

    row = lax.broadcasted_iota(jnp.int32, (B, D), 0)
    lane = lax.broadcasted_iota(jnp.int32, (B, D), 1)

    def column(r):
        return jnp.sum(jnp.where(row == lane, jnp.broadcast_to(r, (B, D)), 0.0), axis=1, keepdims=True)

    lens_row = jnp.concatenate([lens_ref[...].astype(F32), jnp.zeros((1, D - B), F32)], axis=1)
    lens_col = column(lens_row)
    lenb[...] = jnp.broadcast_to(lens_col, (B, D))
    ang = lens_col * inv_ref[...]
    cos_b[...] = jnp.cos(ang)
    sn = jnp.sin(ang)
    sin_b[...] = jnp.where(lane < half, -sn, sn)

    pl.semaphore_wait(barrier, N - 1)

    def rope(t):
        tf = t.astype(F32)
        return (tf * cos_b[...] + pltpu.roll(tf, half, 1) * sin_b[...]).astype(BF16)

    def layer(l, carry):
        for d in range(1, Y):
            t = lax.rem(me_y + d, Y)
            pltpu.make_async_remote_copy(hcur, hbuf.at[l, me_y], bsend.at[l], hrecv.at[l],
                                         device_id=(t, me_x), device_id_type=MESH).start()

        @pl.when(l == 0)
        def _():
            for d in range(1, Y):
                t = lax.rem(me_y + d, Y)
                pltpu.make_async_remote_copy(g_ref, gbuf.at[me_y], bsend.at[L], grecv,
                                             device_id=(t, me_x), device_id_type=MESH).start()

        hf = hcur[...].astype(F32)
        sq = hf * hf
        col = jnp.sum(sq, axis=1, keepdims=True)
        ssown[l] = jnp.sum(jnp.where(row == lane, jnp.broadcast_to(col, (B, D)), 0.0), axis=0, keepdims=True)

        def send_ss(d, carry):
            t = lax.rem(me + d, N)
            pltpu.make_async_remote_copy(ssown.at[l], ssbuf.at[l, d - 1], ssend.at[l], srecv.at[l],
                                         device_id=(lax.div(t, X), lax.rem(t, X)), device_id_type=MESH).start()
            return carry

        lax.fori_loop(1, N, send_ss, 0)
        hbuf[l, me_y] = hcur[...]

        wait_bytes(hbuf.at[l, pl.ds(0, Y - 1)], hrecv.at[l])

        @pl.when(l == 0)
        def _():
            wait_bytes(gbuf.at[pl.ds(0, Y - 1)], grecv)

        wait_bytes(ssbuf.at[l], srecv.at[l])
        tot = jnp.sum(ssbuf[l], axis=0) + ssown[l]
        r = lax.rsqrt(column(tot) / e_total + EPS)
        for j in range(Y):
            gl = gbuf[j, pl.ds(l, 1), :].astype(F32)
            xs[:, j * BLK:(j + 1) * BLK] = (hbuf[l, j].astype(F32) * r * gl).astype(BF16)

        wait_bytes(wqkv_b.at[l], wsem.at[l, 0])
        for i in range(3):
            p = jnp.dot(xs[...], wqkv_b[l, :, i * HD:(i + 1) * HD], preferred_element_type=F32).astype(BF16)
            for j in range(X):
                pq[l, j, :, i * D:(i + 1) * D] = p[:, j * D:(j + 1) * D]
        for d in range(1, X):
            t = lax.rem(me_x + d, X)
            pltpu.make_async_remote_copy(pq.at[l, t], rq.at[l, d - 1], psend.at[l, 0], precv.at[l, 0],
                                         device_id=(me_y, t), device_id_type=MESH).start()
        wait_bytes(win_b.at[l], wsem.at[l, 1])
        for j in range(X):
            pf[l, j] = jnp.dot(xs[...], win_b[l, :, j * FB:(j + 1) * FB], preferred_element_type=F32).astype(BF16)
        for d in range(1, X):
            t = lax.rem(me_x + d, X)
            pltpu.make_async_remote_copy(pf.at[l, t], rf.at[l, d - 1], psend.at[l, 1], precv.at[l, 1],
                                         device_id=(me_y, t), device_id_type=MESH).start()

        wait_bytes(rq.at[l], precv.at[l, 0])
        s = pq[l, me_x].astype(F32)
        for d in range(X - 1):
            s = s + rq[l, d].astype(F32)
        q = rope(s[:, :D].astype(BF16))
        k = rope(s[:, D:2 * D].astype(BF16))
        v = s[:, 2 * D:].astype(BF16)
        q_b[...] = q
        k_out[l] = k
        v_out[l] = v

        wait_bytes(rf.at[l], precv.at[l, 1])
        s = pf[l, me_x].astype(F32)
        for d in range(X - 1):
            s = s + rf[l, d].astype(F32)
        fbuf[l, me_x] = _gelu(s.astype(BF16).astype(F32)).astype(BF16)
        for d in range(1, X):
            t = lax.rem(me_x + d, X)
            pltpu.make_async_remote_copy(fbuf.at[l, me_x], fbuf.at[l, me_x], asend.at[l, 0], arecv.at[l, 0],
                                         device_id=(me_y, t), device_id_type=MESH).start()

        scale = D ** -0.5
        wait_bytes(k_b.at[l], wsem.at[l, 2])
        G = 16
        grow = lax.broadcasted_iota(jnp.int32, (G, S), 0)

        def scores(i, carry):
            b0 = pl.multiple_of(i * G, G)
            qg = q_b[pl.ds(b0, G), :]
            acc = jnp.zeros((G, S), F32)
            for j in range(G):
                t = lax.dot_general(qg, k_b[l, b0 + j], (((1,), (1,)), ((), ())), preferred_element_type=F32)
                acc = jnp.where(grow == j, t, acc)
            sc_b[pl.ds(b0, G), :] = acc
            return carry

        lax.fori_loop(0, B // G, scores, 0)
        sc = sc_b[...] * scale
        pos = lax.broadcasted_iota(jnp.int32, (B, S), 1).astype(F32)
        lc = lenb[...]
        sc = jnp.where(pos < jnp.concatenate([lc] * (S // D), axis=1), sc, -jnp.inf)
        sn = jnp.sum(q.astype(F32) * k.astype(F32), axis=1, keepdims=True) * scale
        m = jnp.maximum(jnp.max(sc, axis=1, keepdims=True), sn)
        p = jnp.exp(sc - m)
        pn = jnp.exp(sn - m)
        den = jnp.sum(p, axis=1, keepdims=True) + pn
        sc_b[...] = p
        wait_bytes(v_b.at[l], wsem.at[l, 3])
        orow = lax.broadcasted_iota(jnp.int32, (G, D), 0)

        def values(i, carry):
            b0 = pl.multiple_of(i * G, G)
            pg = sc_b[pl.ds(b0, G), :].astype(BF16)
            acc = jnp.zeros((G, D), F32)
            for j in range(G):
                t = jnp.dot(pg, v_b[l, b0 + j], preferred_element_type=F32)
                acc = jnp.where(orow == j, t, acc)
            of32[pl.ds(b0, G), :] = acc
            return carry

        lax.fori_loop(0, B // G, values, 0)
        o = of32[...] + pn * v.astype(F32)
        obuf[l, me_x] = (o / den).astype(BF16)
        for d in range(1, X):
            t = lax.rem(me_x + d, X)
            pltpu.make_async_remote_copy(obuf.at[l, me_x], obuf.at[l, me_x], asend.at[l, 1], arecv.at[l, 1],
                                         device_id=(me_y, t), device_id_type=MESH).start()

        wait_bytes(wout_b.at[l], wsem.at[l, 4])
        wait_bytes(fbuf.at[l, pl.ds(0, X - 1)], arecv.at[l, 0])
        wait_bytes(wo_b.at[l], wsem.at[l, 5])
        wait_bytes(obuf.at[l, pl.ds(0, X - 1)], arecv.at[l, 1])
        W = 2 * BLK
        for n in range(Y * BLK // W):
            cols = slice(n * W, (n + 1) * W)
            acc = jnp.zeros((B, W), F32)
            for j in range(X):
                acc = acc + jnp.dot(fbuf[l, j], wout_b[l, j * FB:(j + 1) * FB, cols], preferred_element_type=F32)
                acc = acc + jnp.dot(obuf[l, j], wo_b[l, j * D:(j + 1) * D, cols], preferred_element_type=F32)
            ybuf[l, 2 * n] = acc[:, :BLK].astype(BF16)
            ybuf[l, 2 * n + 1] = acc[:, BLK:].astype(BF16)
        for d in range(1, Y):
            t = lax.rem(me_y + d, Y)
            pltpu.make_async_remote_copy(ybuf.at[l, t], ry.at[l, d - 1], ysend.at[l], yrecv.at[l],
                                         device_id=(t, me_x), device_id_type=MESH).start()
        wait_bytes(ry.at[l], yrecv.at[l])
        y = ybuf[l, me_y].astype(F32)
        for d in range(Y - 1):
            y = y + ry[l, d].astype(F32)
        wait_bytes(hbuf.at[l, pl.ds(0, Y - 1)], bsend.at[l])
        hcur[...] = (hcur[...].astype(F32) + y.astype(BF16).astype(F32)).astype(BF16)
        return carry

    for l in range(L):
        layer(l, 0)
    h_out[...] = hcur[...]

    for l in range(L):
        wait_bytes(ssbuf.at[l], ssend.at[l])
        wait_bytes(rq.at[l], psend.at[l, 0])
        wait_bytes(rf.at[l], psend.at[l, 1])
        wait_bytes(fbuf.at[l, pl.ds(0, X - 1)], asend.at[l, 0])
        wait_bytes(obuf.at[l, pl.ds(0, X - 1)], asend.at[l, 1])
        wait_bytes(ry.at[l], ysend.at[l])
    wait_bytes(gbuf.at[pl.ds(0, Y - 1)], bsend.at[L])


def solution(mesh):
    X = mesh.shape['x']
    Y = mesh.shape['yz']
    act = P(None, ('x', 'yz'))
    w_first = P(None, 'x', 'yz')
    w_second = P(None, 'yz', 'x')
    cache = P(None, None, ('yz', 'x'), None, None)
    new = P(None, None, ('yz', 'x'), None)

    def body(h, g, wq, wk, wv, w_in, wo, w_out, kc, vc, lens):
        B, BLK = h.shape
        L, E, HD = wq.shape
        FL = w_in.shape[2]
        FB = FL // X
        S, D = kc.shape[3], kc.shape[4]
        half = D // 2
        kc = kc.reshape(L, B, S, D)
        vc = vc.reshape(L, B, S, D)
        i = np.arange(half, dtype=np.float32)
        inv = np.power(np.float32(10000.0), -i / np.float32(half)).astype(np.float32)
        inv = jnp.asarray(np.concatenate([inv, inv])[None])
        vm = pl.BlockSpec(memory_space=pltpu.VMEM)
        hbm = pl.BlockSpec(memory_space=pl.ANY)
        N = X * Y
        dma = pltpu.SemaphoreType.DMA
        scratch = [
            pltpu.VMEM((L, E, 3 * HD), BF16), pltpu.VMEM((L, E, FL), BF16),
            pltpu.VMEM((L, HD, E), BF16), pltpu.VMEM((L, FL, E), BF16),
            pltpu.VMEM((L, B, S, D), BF16), pltpu.VMEM((L, B, S, D), BF16),
            pltpu.VMEM((B, BLK), BF16), pltpu.VMEM((L, Y, B, BLK), BF16), pltpu.VMEM((Y, L, BLK), BF16),
            pltpu.VMEM((L, 1, D), F32), pltpu.VMEM((L, N - 1, 1, D), F32), pltpu.VMEM((B, Y * BLK), BF16),
            pltpu.VMEM((B, D), F32), pltpu.VMEM((B, D), F32), pltpu.VMEM((B, D), F32),
            pltpu.VMEM((L, X, B, 3 * D), BF16), pltpu.VMEM((L, X, B, FB), BF16),
            pltpu.VMEM((L, X - 1, B, 3 * D), BF16), pltpu.VMEM((L, X - 1, B, FB), BF16),
            pltpu.VMEM((B, D), BF16), pltpu.VMEM((B, S), F32), pltpu.VMEM((B, D), F32),
            pltpu.VMEM((L, X, B, D), BF16), pltpu.VMEM((L, X, B, FB), BF16),
            pltpu.VMEM((L, Y, B, BLK), BF16), pltpu.VMEM((L, Y - 1, B, BLK), BF16),
            dma((L, 6)), dma((L + 1,)), dma((L,)), dma, dma((L,)), dma((L,)),
            dma((L, 2)), dma((L, 2)), dma((L, 2)), dma((L, 2)), dma((L,)), dma((L,)),
        ]
        h_new, k_new, v_new = pl.pallas_call(
            functools.partial(_kernel, X, Y, float(BLK * N)),
            out_shape=(jax.ShapeDtypeStruct((B, BLK), BF16),
                       jax.ShapeDtypeStruct((L, B, D), BF16),
                       jax.ShapeDtypeStruct((L, B, D), BF16)),
            in_specs=[vm] * 4 + [hbm] * 8,
            out_specs=(vm, vm, vm),
            scratch_shapes=scratch,
            compiler_params=pltpu.CompilerParams(
                collective_id=0, has_side_effects=True, vmem_limit_bytes=67043328),
            name="decode_step",
        )(h, g, lens.reshape(1, B), inv, wq, wk, wv, w_in, wo, w_out, kc, vc)
        return h_new, k_new.reshape(L, B, 1, D), v_new.reshape(L, B, 1, D)

    return jax.shard_map(
        body, mesh=mesh,
        in_specs=(act, act, w_first, w_first, w_first, w_first, w_second, w_second, cache, cache, P(None)),
        out_specs=(act, new, new), check_vma=False)
```

time: 387 us -> 62.5 us (0.16)
  waiting for transfers between devices: 165 us -> 0 us
  blocking collectives: 155 us -> 0 us
  Pallas kernels: 0 us -> 57.5 us
  matrix products: 34.3 us -> 0 us
  between operations: 14.1 us -> 0.64 us
  other arithmetic: 13 us -> 0 us
    unnamed x6 -> x0, waiting for transfers between devices: 124 us -> none
    psum x2 -> x0, blocking collectives: 82.1 us -> none  [body(): ss = lax.psum(jnp.sum(hf * hf, axis=-1, keepdims=True), ('yz', 'x'))]
    all_gather x4 -> x0, blocking collectives: 73.4 us -> none  [the longest x2 61.4 us: body(): xg = lax.all_gather(x, 'yz', axis=1, tiled=True)]
    pallas_call x0 -> x1, Pallas kernels: none -> 57.5 us  [body(): pl.pallas_call(functools.partial(_kernel, X, Y, float(BLK * N)), out_shap...]
    reduce_scatter x2 -> x0, waiting for transfers between devices: 40.8 us -> none  [body(): lax.psum_scatter(jnp.concatenate(parts, axis=2), 'x', scatter_dimension=1...]
    dot_general x16 -> x0, matrix products: 34.3 us -> none  [the longest x8 15.2 us: body(): jnp.dot(xg, w[l], preferred_element_type=jnp.float32).astype(jnp.bfloat16)]
    convert_element_type x8 -> x0, other arithmetic: 5.06 us -> none  [the longest x2 1.78 us: body(): jax.nn.gelu(r[:, 3 * hdn:].astype(jnp.float32), approximate=True)]
  transfers between devices with their start and end apart: 4 -> 0, of which waited for: 4 -> 0; matrix products, arithmetic and copies ran while one was open for 0% -> 0% of each run, Pallas kernels for 0% -> 0%
where the time goes in v1:
time: 62.5 us; the launch traced here: 62.2 us
  Pallas kernels  57.5 us (92%)
  local copies, waits for them, and re-layouts  4.07 us (7%)
  between operations  0.64 us (1%)
    pallas_call x1, Pallas kernels, body(): pl.pallas_call(functools.partial(_kernel, X, Y, float(BLK * N)), out_shap...  57.5 us
    unnamed x3, local copies, waits for them, and re-layouts  4.07 us

profile of v1, /device:TPU:0, one launch (start us, length us, event | category | flops | bytes accessed | tf_op | source)
XLA Modules:
  0.0 62.2 jit_solution(3182506934074868942)
XLA Ops:
  0.6 57.5 %decode_step.1 = (bf16[64,128]{1,0:T(8,128)(2,1)}, bf16[2,64,128]{2,1,0:T(8,128)(2,1)}, bf16[2,64,128]{2,1,0:T(8,128)(2,1)}) custom-call(bf16[64,128]{1,0:T(8,128)(2,1)} %h_ref.1, bf16[2,128]{1,0:T(2,128)(2,1)} %g_ref.1, s32[1,64]{1,0:T(1,128)} %bitcast.13, f32[1,128]{1,0:T(1,128)} %constant.2.clone.inv_ref, bf16[2,1024,512]{2,1,0:T(8,128)(2,1)} %wq.1, ...), custom_call_target="tpu_custom_call" | custom-call | tf_op jit(solution)/shard_map/decode_step/pallas_call | solution.py:307
  58.1 1.3 %copy.20 = bf16[64,128]{1,0:T(8,128)(2,1)} copy(bf16[64,128]{1,0:T(8,128)(2,1)} %get-tuple-element.15) | data formatting | bytes 32768
  59.4 1.4 %copy.21 = bf16[2,64,1,128]{3,1,2,0:T(8,128)(2,1)} copy(bf16[2,64,1,128]{3,1,2,0:T(8,128)(2,1)} %bitcast.12) | data formatting | bytes 65536
  60.8 1.4 %copy.22 = bf16[2,64,1,128]{3,1,2,0:T(8,128)(2,1)} copy(bf16[2,64,1,128]{3,1,2,0:T(8,128)(2,1)} %bitcast.11) | data formatting | bytes 65536

commit v2 on v1

v2 whole, which is shorter than its diff:
```python
import functools
import math

import numpy as np

import jax
import jax.numpy as jnp
from jax import lax
from jax.experimental import pallas as pl
from jax.experimental.pallas import tpu as pltpu
from jax.sharding import PartitionSpec as P

EPS = 1e-6
MESH = pl.DeviceIdType.MESH
F32 = jnp.float32
BF16 = jnp.bfloat16
CH = 2


def _gelu(x):
    return 0.5 * x * (1.0 + jnp.tanh(math.sqrt(2.0 / math.pi) * (x + 0.044715 * (x * x * x))))


def _partner(i, mask):
    bit = 1
    t = i
    while bit <= mask:
        if mask & bit:
            t = t + bit * (1 - 2 * lax.rem(lax.div(i, bit), 2))
        bit *= 2
    return t


def _kernel(X, Y, e_total, h_ref, g_ref, lens_ref, inv_ref, wq, wk, wv, w_in, wo, w_out, kc, vc,
            h_out, k_out, v_out,
            wqkv_b, win_b, wo_b, wout_b, k_b, v_b,
            hcur, hbuf, gown, gbuf, lens_b, inv_b, ssown, ssbuf, xs, cos_b, sin_b, lenb,
            pq, pkv, rq, rkv, q_b, sc_b, of32, obuf,
            fsib, fsibr, fown, fcross, fcrossr, fbuf, yacc, ybuf, ry,
            isem, wsem, hsend, hrecv, gsend, grecv, ssend, srecv, qsend, qrecv,
            asend, arecv, bsend, brecv, csend, crecv, osend, orecv, ysend, yrecv):
    me_y = lax.axis_index("yz")
    me_x = lax.axis_index("x")
    me = me_y * X + me_x
    N = X * Y
    L = wqkv_b.shape[0]
    B, BLK = h_ref.shape
    S, D = kc.shape[2], kc.shape[3]
    E = wq.shape[1]
    HD = wq.shape[2]
    FL = w_in.shape[2]
    FH = FL // 2
    CW = FH // CH
    half = D // 2
    core = lax.rem(me_x, 2)
    sib = _partner(me_x, 1)
    cross = _partner(me_x, 2)
    masks = list(range(Y - 1, 0, -1))

    def remote(src, dst, send, recv, y, x):
        pltpu.make_async_remote_copy(src, dst, send, recv, device_id=(y, x), device_id_type=MESH).start()

    def wait_bytes(ref, sem, name="wait"):
        with jax.named_scope(name):
            pltpu.make_async_copy(ref, ref, sem).wait()

    inputs = [pltpu.make_async_copy(s, d, isem.at[i]) for i, (s, d) in enumerate(
        ((h_ref, hcur), (g_ref, gown), (lens_ref, lens_b), (inv_ref, inv_b)))]
    for c in inputs:
        c.start()

    barrier = pltpu.get_barrier_semaphore()

    def greet(d, carry):
        t = lax.rem(me + d, N)
        pl.semaphore_signal(barrier, inc=1, device_id=(lax.div(t, X), lax.rem(t, X)), device_id_type=MESH)
        return carry

    lax.fori_loop(1, N, greet, 0)

    def load(l):
        for i, w in enumerate((wq, wk, wv)):
            pltpu.make_async_copy(w.at[l], wqkv_b.at[l, :, pl.ds(i * HD, HD)], wsem.at[l, 0]).start()
        for i, (w, b) in enumerate(((w_in, win_b), (kc, k_b), (vc, v_b), (w_out, wout_b))):
            n = w.shape[1] // 4
            for j in range(4):
                rows = pl.ds(j * n, n)
                pltpu.make_async_copy(w.at[l, rows], b.at[l, rows], wsem.at[l, i + 1]).start()
        pltpu.make_async_copy(wo.at[l], wo_b.at[l], wsem.at[l, 5]).start()

    for c in inputs:
        c.wait()
    for l in range(L):
        load(l)
    gbuf[me_y] = gown[...]

    row = lax.broadcasted_iota(jnp.int32, (B, D), 0)
    lane = lax.broadcasted_iota(jnp.int32, (B, D), 1)

    def column(r):
        return jnp.sum(jnp.where(row == lane, jnp.broadcast_to(r, (B, D)), 0.0), axis=1, keepdims=True)

    def as_row(c):
        return jnp.sum(jnp.where(row == lane, jnp.broadcast_to(c, (B, D)), 0.0), axis=0, keepdims=True)

    lens_row = jnp.concatenate([lens_b[...].astype(F32), jnp.zeros((1, D - B), F32)], axis=1)
    lens_col = column(lens_row)
    lenb[...] = jnp.broadcast_to(lens_col, (B, D))
    ang = lens_col * inv_b[...]
    cos_b[...] = jnp.cos(ang)
    sn = jnp.sin(ang)
    sin_b[...] = jnp.where(lane < half, -sn, sn)

    def rope(t):
        tf = t.astype(F32)
        return (tf * cos_b[...] + pltpu.roll(tf, half, 1) * sin_b[...]).astype(BF16)

    def send_h(l):
        for m in masks:
            remote(hcur, hbuf.at[l, me_y], hsend.at[l], hrecv.at[l], _partner(me_y, m), me_x)
        hf = hcur[...].astype(F32)
        ssown[l] = as_row(jnp.sum(hf * hf, axis=1, keepdims=True))

        def send_ss(d, carry):
            t = lax.rem(me + d, N)
            remote(ssown.at[l], ssbuf.at[l, d - 1], ssend.at[l], srecv.at[l], lax.div(t, X), lax.rem(t, X))
            return carry

        lax.fori_loop(1, N, send_ss, 0)
        hbuf[l, me_y] = hcur[...]

    with jax.named_scope("w_bar"):
        pl.semaphore_wait(barrier, N - 1)
    for m in masks:
        remote(gown, gbuf.at[me_y], gsend, grecv, _partner(me_y, m), me_x)

    for l in range(L):
        send_h(l)
        if l == 0:
            wait_bytes(gbuf.at[pl.ds(0, Y - 1)], grecv)
        wait_bytes(hbuf.at[l, pl.ds(0, Y - 1)], hrecv.at[l], "w_h")
        wait_bytes(ssbuf.at[l], srecv.at[l], "w_ss")
        tot = jnp.sum(ssbuf[l], axis=0) + ssown[l]
        r = lax.rsqrt(column(tot) / e_total + EPS)
        for j in range(Y):
            gl = gbuf[j, pl.ds(l, 1), :].astype(F32)
            xs[:, j * BLK:(j + 1) * BLK] = (hbuf[l, j].astype(F32) * r * gl).astype(BF16)

        wait_bytes(wqkv_b.at[l], wsem.at[l, 0], "w_wqkv")

        def part(i):
            return jnp.dot(xs[...], wqkv_b[l, :, i * HD:(i + 1) * HD], preferred_element_type=F32).astype(BF16)

        p = part(0)
        for j in range(X):
            pq[l, j] = p[:, j * D:(j + 1) * D]
        for m in (2, 3, 1):
            t = _partner(me_x, m)
            remote(pq.at[l, t], rq.at[l, m - 1], qsend.at[l, 0], qrecv.at[l, 0], me_y, t)
        for i in range(2):
            p = part(i + 1)
            for j in range(X):
                pkv[l, j, :, i * D:(i + 1) * D] = p[:, j * D:(j + 1) * D]
        for m in (2, 3, 1):
            t = _partner(me_x, m)
            remote(pkv.at[l, t], rkv.at[l, m - 1], qsend.at[l, 1], qrecv.at[l, 1], me_y, t)

        wait_bytes(win_b.at[l], wsem.at[l, 1], "w_win")
        for i in range(CH):
            cols = pl.ds(pl.multiple_of((1 - core) * FH + i * CW, CW), CW)
            fsib[l, i] = jnp.dot(xs[...], win_b[l, :, cols], preferred_element_type=F32).astype(BF16)
            remote(fsib.at[l, i], fsibr.at[l, i], asend.at[l, i], arecv.at[l, i], me_y, sib)
        for i in range(CH):
            cols = pl.ds(pl.multiple_of(core * FH + i * CW, CW), CW)
            fown[i] = jnp.dot(xs[...], win_b[l, :, cols], preferred_element_type=F32)
        for i in range(CH):
            wait_bytes(fsibr.at[l, i], arecv.at[l, i], "w_fs")
            s = fown[i] + fsibr[l, i].astype(F32)
            fown[i] = s
            fcross[l, i] = s.astype(BF16)
            remote(fcross.at[l, i], fcrossr.at[l, i], bsend.at[l, i], brecv.at[l, i], me_y, cross)

        scale = D ** -0.5
        wait_bytes(k_b.at[l], wsem.at[l, 2], "w_k")
        wait_bytes(rq.at[l], qrecv.at[l, 0], "w_q")
        s = pq[l, me_x].astype(F32)
        for d in range(X - 1):
            s = s + rq[l, d].astype(F32)
        q = rope(s.astype(BF16))
        q_b[...] = q
        G = 16
        grow = lax.broadcasted_iota(jnp.int32, (G, S), 0)
        for i in range(B // G):
            b0 = i * G
            qg = q_b[b0:b0 + G, :]
            acc = jnp.zeros((G, S), F32)
            for j in range(G):
                t = lax.dot_general(qg, k_b[l, b0 + j], (((1,), (1,)), ((), ())), preferred_element_type=F32)
                acc = jnp.where(grow == j, t, acc)
            sc_b[b0:b0 + G, :] = acc
        wait_bytes(rkv.at[l], qrecv.at[l, 1], "w_kv")
        s = pkv[l, me_x].astype(F32)
        for d in range(X - 1):
            s = s + rkv[l, d].astype(F32)
        k = rope(s[:, :D].astype(BF16))
        v = s[:, D:].astype(BF16)
        k_out[l] = k
        v_out[l] = v
        sc = sc_b[...] * scale
        pos = lax.broadcasted_iota(jnp.int32, (B, S), 1).astype(F32)
        sc = jnp.where(pos < jnp.concatenate([lenb[...]] * (S // D), axis=1), sc, -jnp.inf)
        sn = jnp.sum(q.astype(F32) * k.astype(F32), axis=1, keepdims=True) * scale
        m = jnp.maximum(jnp.max(sc, axis=1, keepdims=True), sn)
        p = jnp.exp(sc - m)
        pn = jnp.exp(sn - m)
        den = jnp.sum(p, axis=1, keepdims=True) + pn
        sc_b[...] = p
        wait_bytes(v_b.at[l], wsem.at[l, 3], "w_v")
        orow = lax.broadcasted_iota(jnp.int32, (G, D), 0)
        for i in range(B // G):
            b0 = i * G
            pg = sc_b[b0:b0 + G, :].astype(BF16)
            acc = jnp.zeros((G, D), F32)
            for j in range(G):
                t = jnp.dot(pg, v_b[l, b0 + j], preferred_element_type=F32)
                acc = jnp.where(orow == j, t, acc)
            of32[b0:b0 + G, :] = acc
        o = of32[...] + pn * v.astype(F32)
        obuf[l, me_x] = (o / den).astype(BF16)
        for m in (2, 3, 1):
            t = _partner(me_x, m)
            remote(obuf.at[l, me_x], obuf.at[l, me_x], osend.at[l], orecv.at[l], me_y, t)

        for i in range(CH):
            wait_bytes(fcrossr.at[l, i], brecv.at[l, i], "w_fc")
            s = fown[i] + fcrossr[l, i].astype(F32)
            c = core * CH + i
            fbuf[l, c] = _gelu(s.astype(BF16).astype(F32)).astype(BF16)
            remote(fbuf.at[l, c], fbuf.at[l, c], csend.at[l, i], crecv.at[l, i], me_y, sib)

        wait_bytes(wout_b.at[l], wsem.at[l, 4], "w_wout")

        def f_dot(c0):
            f = jnp.concatenate([fbuf[l, c0 + i] for i in range(CH)], axis=1)
            rows = pl.ds(pl.multiple_of(c0 * CW, CW), FH)
            return jnp.dot(f, wout_b[l, rows, :], preferred_element_type=F32)

        yacc[...] = f_dot(core * CH)
        for i in range(CH):
            wait_bytes(fbuf.at[l, i], crecv.at[l, i], "w_fg")
        yacc[...] = yacc[...] + f_dot((1 - core) * CH)
        wait_bytes(wo_b.at[l], wsem.at[l, 5], "w_wo")
        wait_bytes(obuf.at[l, pl.ds(0, X - 1)], orecv.at[l], "w_og")
        og = jnp.concatenate([obuf[l, j] for j in range(X)], axis=1)
        for m in masks[::2]:
            z = lax.div(_partner(me_y, m), 2)
            cols = pl.ds(pl.multiple_of(z * 2 * BLK, 2 * BLK), 2 * BLK)
            acc = yacc[:, cols] + jnp.dot(og, wo_b[l, :, cols], preferred_element_type=F32)
            ybuf[l, 2 * z] = acc[:, :BLK].astype(BF16)
            ybuf[l, 2 * z + 1] = acc[:, BLK:].astype(BF16)
            for n in (m, m - 1) if m > 1 else (m,):
                t = _partner(me_y, n)
                remote(ybuf.at[l, t], ry.at[l, n - 1], ysend.at[l], yrecv.at[l], t, me_x)
        wait_bytes(hbuf.at[l, pl.ds(0, Y - 1)], hsend.at[l])
        wait_bytes(ry.at[l], yrecv.at[l], "w_y")
        y = ybuf[l, me_y].astype(F32)
        for d in range(Y - 1):
            y = y + ry[l, d].astype(F32)
        hcur[...] = (hcur[...].astype(F32) + y.astype(BF16).astype(F32)).astype(BF16)
    h_out[...] = hcur[...]

    for l in range(L):
        wait_bytes(ssbuf.at[l], ssend.at[l])
        wait_bytes(rq.at[l], qsend.at[l, 0])
        wait_bytes(rkv.at[l], qsend.at[l, 1])
        for i in range(CH):
            wait_bytes(fsib.at[l, i], asend.at[l, i])
            wait_bytes(fcross.at[l, i], bsend.at[l, i])
            wait_bytes(fbuf.at[l, i], csend.at[l, i])
        wait_bytes(obuf.at[l, pl.ds(0, X - 1)], osend.at[l])
        wait_bytes(ry.at[l], ysend.at[l])
    wait_bytes(gbuf.at[pl.ds(0, Y - 1)], gsend)


def _finish(h, k, v, h_out, k_out, v_out, sem):
    copies = [pltpu.make_async_copy(a, b, sem.at[i]) for i, (a, b) in enumerate(((k, k_out), (v, v_out), (h, h_out)))]
    for c in copies:
        c.start()
    for c in copies:
        c.wait()


def solution(mesh):
    X = mesh.shape['x']
    Y = mesh.shape['yz']
    act = P(None, ('x', 'yz'))
    w_first = P(None, 'x', 'yz')
    w_second = P(None, 'yz', 'x')
    cache = P(None, None, ('yz', 'x'), None, None)
    new = P(None, None, ('yz', 'x'), None)

    def body(h, g, wq, wk, wv, w_in, wo, w_out, kc, vc, lens):
        B, BLK = h.shape
        L, E, HD = wq.shape
        FL = w_in.shape[2]
        S, D = kc.shape[3], kc.shape[4]
        half = D // 2
        CW = FL // 2 // CH
        kc = kc.reshape(L, B, S, D)
        vc = vc.reshape(L, B, S, D)
        i = np.arange(half, dtype=np.float32)
        inv = np.power(np.float32(10000.0), -i / np.float32(half)).astype(np.float32)
        inv = jnp.asarray(np.concatenate([inv, inv])[None])
        vm = pl.BlockSpec(memory_space=pltpu.VMEM)
        hbm = pl.BlockSpec(memory_space=pl.ANY)
        far = pl.BlockSpec(memory_space=pltpu.HBM)
        N = X * Y
        dma = pltpu.SemaphoreType.DMA
        V = pltpu.VMEM
        scratch = [
            V((L, E, 3 * HD), BF16), V((L, E, FL), BF16), V((L, HD, E), BF16), V((L, FL, E), BF16),
            V((L, B, S, D), BF16), V((L, B, S, D), BF16),
            V((B, BLK), BF16), V((L, Y, B, BLK), BF16), V((L, BLK), BF16), V((Y, L, BLK), BF16),
            V((1, B), jnp.int32), V((1, D), F32),
            V((L, 1, D), F32), V((L, N - 1, 1, D), F32), V((B, Y * BLK), BF16),
            V((B, D), F32), V((B, D), F32), V((B, D), F32),
            V((L, X, B, D), BF16), V((L, X, B, 2 * D), BF16),
            V((L, X - 1, B, D), BF16), V((L, X - 1, B, 2 * D), BF16),
            V((B, D), BF16), V((B, S), F32), V((B, D), F32), V((L, X, B, D), BF16),
            V((L, CH, B, CW), BF16), V((L, CH, B, CW), BF16), V((CH, B, CW), F32),
            V((L, CH, B, CW), BF16), V((L, CH, B, CW), BF16), V((L, 2 * CH, B, CW), BF16),
            V((B, Y * BLK), F32), V((L, Y, B, BLK), BF16), V((L, Y - 1, B, BLK), BF16),
            dma((4,)), dma((L, 6)), dma((L,)), dma((L,)), dma, dma, dma((L,)), dma((L,)), dma((L, 2)), dma((L, 2)),
            dma((L, CH)), dma((L, CH)), dma((L, CH)), dma((L, CH)), dma((L, CH)), dma((L, CH)),
            dma((L,)), dma((L,)), dma((L,)), dma((L,)),
        ]
        shapes = (jax.ShapeDtypeStruct((B, BLK), BF16),
                  jax.ShapeDtypeStruct((L, B, D), BF16),
                  jax.ShapeDtypeStruct((L, B, D), BF16))
        outs = pl.pallas_call(
            functools.partial(_kernel, X, Y, float(BLK * N)),
            out_shape=tuple(V(t.shape, t.dtype) for t in shapes),
            in_specs=[hbm] * 12,
            out_specs=(vm, vm, vm),
            scratch_shapes=scratch,
            compiler_params=pltpu.CompilerParams(
                collective_id=0, has_side_effects=True, vmem_limit_bytes=56 * 1024 * 1024),
            name="decode_step",
        )(h, g, lens.reshape(1, B), inv, wq, wk, wv, w_in, wo, w_out, kc, vc)
        h_new, k_new, v_new = pl.pallas_call(
            _finish, out_shape=shapes, in_specs=[vm] * 3, out_specs=(far, far, far), name="finish",
            scratch_shapes=[dma((3,))],
        )(*[pltpu.with_memory_space_constraint(t, pltpu.VMEM) for t in outs])
        return h_new, k_new.reshape(L, B, 1, D), v_new.reshape(L, B, 1, D)

    return jax.shard_map(
        body, mesh=mesh,
        in_specs=(act, act, w_first, w_first, w_first, w_first, w_second, w_second, cache, cache, P(None)),
        out_specs=(act, new, new), check_vma=False)
```

time: 62.5 us -> 50 us (0.80)
  Pallas kernels: 57.5 us -> 49.2 us
  local copies, waits for them, and re-layouts: 4.07 us -> 0 us
    pallas_call x1, Pallas kernels: 57.5 us -> 48.5 us  [body(): pl.pallas_call(functools.partial(_kernel, X, Y, float(BLK * N)), out_shap...]
    unnamed x3 -> x0, local copies, waits for them, and re-layouts: 4.07 us -> none
    pallas_call x0 -> x1, Pallas kernels: none -> 0.66 us  [body(): pl.pallas_call(_finish, out_shape=shapes, in_specs=[vm] * 3, out_specs=(f...]
where the time goes in v2:
time: 50 us; the launch traced here: 49.8 us
  Pallas kernels  49.2 us (98%)
  between operations  0.64 us (1%)
    pallas_call x1, Pallas kernels, body(): pl.pallas_call(functools.partial(_kernel, X, Y, float(BLK * N)), out_shap...  48.5 us

profile of v2, /device:TPU:0, one launch (start us, length us, event | category | flops | bytes accessed | tf_op | source)
XLA Modules:
  0.0 49.8 jit_solution(4946068691831467891)
XLA Ops:
  0.6 48.5 %decode_step.1 = (bf16[64,128]{1,0:T(8,128)(2,1)S(1)}, bf16[2,64,128]{2,1,0:T(8,128)(2,1)S(1)}, bf16[2,64,128]{2,1,0:T(8,128)(2,1)S(1)}) custom-call(bf16[64,128]{1,0:T(8,128)(2,1)} %h_ref.1, bf16[2,128]{1,0:T(2,128)(2,1)} %g_ref.1, s32[1,64]{1,0:T(1,128)} %bitcast.11, f32[1,128]{1,0:T(1,128)} %constant.2.clone.inv_ref, bf16[2,1024,512]{2,1,0:T(8,128)(2,1)} %wq.1, ...), custom_call_target="tpu_custom_call" | custom-call | tf_op jit(solution)/shard_map/decode_step/pallas_call | solution.py:340
  49.1 0.7 %finish.1 = (bf16[64,128]{1,0:T(8,128)(2,1)}, bf16[2,64,128]{2,1,0:T(8,128)(2,1)}, bf16[2,64,128]{2,1,0:T(8,128)(2,1)}) custom-call(bf16[64,128]{1,0:T(8,128)(2,1)S(1)} %get-tuple-element.9.h, bf16[2,64,128]{2,1,0:T(8,128)(2,1)S(1)} %get-tuple-element.10.k, bf16[2,64,128]{2,1,0:T(8,128)(2,1)S(1)} %get-tuple-element.11.v), custom_call_target="tpu_custom_call" | custom-call | tf_op jit(solution)/shard_map/finish/pallas_call | solution.py:350

commit v3 on v2

--- a/solution.py
+++ b/solution.py
@@ -33,9 +33,9 @@
 
 def _kernel(X, Y, e_total, h_ref, g_ref, lens_ref, inv_ref, wq, wk, wv, w_in, wo, w_out, kc, vc,
             h_out, k_out, v_out,
-            wqkv_b, win_b, wo_b, wout_b, k_b, v_b,
+            wqkv_b, win_b, wo_b, wout_b, k_b, v_b, kt_b,
             hcur, hbuf, gown, gbuf, lens_b, inv_b, ssown, ssbuf, xs, cos_b, sin_b, lenb,
-            pq, pkv, rq, rkv, q_b, sc_b, of32, obuf,
+            pq, pkv, rq, rkv, q_b, m_b, d_b, of32, obuf,
             fsib, fsibr, fown, fcross, fcrossr, fbuf, yacc, ybuf, ry,
             isem, wsem, hsend, hrecv, gsend, grecv, ssend, srecv, qsend, qrecv,
             asend, arecv, bsend, brecv, csend, crecv, osend, orecv, ysend, yrecv):
@@ -53,9 +53,11 @@
     CW = FH // CH
     half = D // 2
     core = lax.rem(me_x, 2)
-    sib = _partner(me_x, 1)
-    cross = _partner(me_x, 2)
+    py = [_partner(me_y, m) for m in range(Y)]
+    px = [_partner(me_x, m) for m in range(X)]
+    sib, cross = px[1], px[2]
     masks = list(range(Y - 1, 0, -1))
+    others = [(m, n) for m in range(Y - 1, -1, -1) for n in range(X - 1, 0, -1)]
 
     def remote(src, dst, send, recv, y, x):
         pltpu.make_async_remote_copy(src, dst, send, recv, device_id=(y, x), device_id_type=MESH).start()
@@ -79,14 +81,29 @@
     lax.fori_loop(1, N, greet, 0)
 
     def load(l):
+        def rows(w, b, i, parts=4):
+            n = w.shape[1] // parts
+            for j in range(parts):
+                pltpu.make_async_copy(w.at[l, pl.ds(j * n, n)], b.at[l, pl.ds(j * n, n)], wsem.at[l, i]).start()
+
+        rows(kc, k_b, 2)
         for i, w in enumerate((wq, wk, wv)):
             pltpu.make_async_copy(w.at[l], wqkv_b.at[l, :, pl.ds(i * HD, HD)], wsem.at[l, 0]).start()
-        for i, (w, b) in enumerate(((w_in, win_b), (kc, k_b), (vc, v_b), (w_out, wout_b))):
-            n = w.shape[1] // 4
-            for j in range(4):
-                rows = pl.ds(j * n, n)
-                pltpu.make_async_copy(w.at[l, rows], b.at[l, rows], wsem.at[l, i + 1]).start()
-        pltpu.make_async_copy(wo.at[l], wo_b.at[l], wsem.at[l, 5]).start()
+        rows(w_in, win_b, 1)
+        rows(vc, v_b, 3)
+        rows(w_out, wout_b, 4)
+        rows(wo, wo_b, 5, 1)
+
+    def transpose_k(l):
+        wait_bytes(k_b.at[l], wsem.at[l, 2], "w_k")
+
+        def step(i, carry):
+            for j in range(8):
+                kt_b[i * 8 + j] = k_b[l, i * 8 + j].T
+            return carry
+
+        with jax.named_scope("kt"):
+            lax.fori_loop(0, B // 8, step, 0)
 
     for c in inputs:
         c.wait()
@@ -116,32 +133,32 @@
         return (tf * cos_b[...] + pltpu.roll(tf, half, 1) * sin_b[...]).astype(BF16)
 
     def send_h(l):
-        for m in masks:
-            remote(hcur, hbuf.at[l, me_y], hsend.at[l], hrecv.at[l], _partner(me_y, m), me_x)
         hf = hcur[...].astype(F32)
         ssown[l] = as_row(jnp.sum(hf * hf, axis=1, keepdims=True))
-
-        def send_ss(d, carry):
-            t = lax.rem(me + d, N)
-            remote(ssown.at[l], ssbuf.at[l, d - 1], ssend.at[l], srecv.at[l], lax.div(t, X), lax.rem(t, X))
-            return carry
-
-        lax.fori_loop(1, N, send_ss, 0)
+        for i, (m, n) in enumerate(others):
+            remote(ssown.at[l], ssbuf.at[l, i], ssend.at[l], srecv.at[l], py[m], px[n])
+        for m in masks:
+            remote(hcur, hbuf.at[l, me_y], hsend.at[l], hrecv.at[l], py[m], me_x)
         hbuf[l, me_y] = hcur[...]
 
     with jax.named_scope("w_bar"):
         pl.semaphore_wait(barrier, N - 1)
     for m in masks:
-        remote(gown, gbuf.at[me_y], gsend, grecv, _partner(me_y, m), me_x)
+        remote(gown, gbuf.at[me_y], gsend, grecv, py[m], me_x)
 
     for l in range(L):
         send_h(l)
         if l == 0:
+            transpose_k(0)
             wait_bytes(gbuf.at[pl.ds(0, Y - 1)], grecv)
         wait_bytes(hbuf.at[l, pl.ds(0, Y - 1)], hrecv.at[l], "w_h")
         wait_bytes(ssbuf.at[l], srecv.at[l], "w_ss")
-        tot = jnp.sum(ssbuf[l], axis=0) + ssown[l]
-        r = lax.rsqrt(column(tot) / e_total + EPS)
+        row_ss = jnp.zeros((B, BLK), F32)
+        for j in range(Y):
+            hf = hbuf[l, j].astype(F32)
+            row_ss = row_ss + hf * hf
+        tot = jnp.sum(row_ss, axis=1, keepdims=True) + column(jnp.sum(ssbuf[l], axis=0))
+        r = lax.rsqrt(tot / e_total + EPS)
         for j in range(Y):
             gl = gbuf[j, pl.ds(l, 1), :].astype(F32)
             xs[:, j * BLK:(j + 1) * BLK] = (hbuf[l, j].astype(F32) * r * gl).astype(BF16)
@@ -155,14 +172,14 @@
         for j in range(X):
             pq[l, j] = p[:, j * D:(j + 1) * D]
         for m in (2, 3, 1):
-            t = _partner(me_x, m)
+            t = px[m]
             remote(pq.at[l, t], rq.at[l, m - 1], qsend.at[l, 0], qrecv.at[l, 0], me_y, t)
         for i in range(2):
             p = part(i + 1)
             for j in range(X):
                 pkv[l, j, :, i * D:(i + 1) * D] = p[:, j * D:(j + 1) * D]
         for m in (2, 3, 1):
-            t = _partner(me_x, m)
+            t = px[m]
             remote(pkv.at[l, t], rkv.at[l, m - 1], qsend.at[l, 1], qrecv.at[l, 1], me_y, t)
 
         wait_bytes(win_b.at[l], wsem.at[l, 1], "w_win")
@@ -181,7 +198,7 @@
             remote(fcross.at[l, i], fcrossr.at[l, i], bsend.at[l, i], brecv.at[l, i], me_y, cross)
 
         scale = D ** -0.5
-        wait_bytes(k_b.at[l], wsem.at[l, 2], "w_k")
+        wait_bytes(v_b.at[l], wsem.at[l, 3], "w_v")
         wait_bytes(rq.at[l], qrecv.at[l, 0], "w_q")
         s = pq[l, me_x].astype(F32)
         for d in range(X - 1):
@@ -190,14 +207,38 @@
         q_b[...] = q
         G = 16
         grow = lax.broadcasted_iota(jnp.int32, (G, S), 0)
-        for i in range(B // G):
+        orow = lax.broadcasted_iota(jnp.int32, (G, D), 0)
+        pos = lax.broadcasted_iota(jnp.int32, (G, S), 1).astype(F32)
+
+        def scores(i):
             b0 = i * G
             qg = q_b[b0:b0 + G, :]
             acc = jnp.zeros((G, S), F32)
             for j in range(G):
-                t = lax.dot_general(qg, k_b[l, b0 + j], (((1,), (1,)), ((), ())), preferred_element_type=F32)
-                acc = jnp.where(grow == j, t, acc)
-            sc_b[b0:b0 + G, :] = acc
+                acc = jnp.where(grow == j, jnp.dot(qg, kt_b[b0 + j], preferred_element_type=F32), acc)
+            ln = lenb[b0:b0 + G, :]
+            sc = jnp.where(pos < jnp.concatenate([ln] * (S // D), axis=1), acc * scale, -jnp.inf)
+            m = jnp.max(sc, axis=1, keepdims=True)
+            p = jnp.exp(sc - m)
+            m_b[b0:b0 + G, :] = jnp.broadcast_to(m, (G, D))
+            d_b[b0:b0 + G, :] = jnp.broadcast_to(jnp.sum(p, axis=1, keepdims=True), (G, D))
+            return p.astype(BF16)
+
+        def values(i, p):
+            b0 = i * G
+            acc = jnp.zeros((G, D), F32)
+            for j in range(G):
+                acc = jnp.where(orow == j, jnp.dot(p, v_b[l, b0 + j], preferred_element_type=F32), acc)
+            of32[b0:b0 + G, :] = acc
+
+        with jax.named_scope("attn"):
+            prev = scores(0)
+            for i in range(1, B // G):
+                cur = scores(i)
+                values(i - 1, prev)
+                prev = cur
+            values(B // G - 1, prev)
+
         wait_bytes(rkv.at[l], qrecv.at[l, 1], "w_kv")
         s = pkv[l, me_x].astype(F32)
         for d in range(X - 1):
@@ -206,29 +247,15 @@
         v = s[:, D:].astype(BF16)
         k_out[l] = k
         v_out[l] = v
-        sc = sc_b[...] * scale
-        pos = lax.broadcasted_iota(jnp.int32, (B, S), 1).astype(F32)
-        sc = jnp.where(pos < jnp.concatenate([lenb[...]] * (S // D), axis=1), sc, -jnp.inf)
-        sn = jnp.sum(q.astype(F32) * k.astype(F32), axis=1, keepdims=True) * scale
-        m = jnp.maximum(jnp.max(sc, axis=1, keepdims=True), sn)
-        p = jnp.exp(sc - m)
+        sn = jnp.sum(q_b[...].astype(F32) * k.astype(F32), axis=1, keepdims=True) * scale
+        m = jnp.maximum(m_b[...], sn)
+        al = jnp.exp(m_b[...] - m)
         pn = jnp.exp(sn - m)
-        den = jnp.sum(p, axis=1, keepdims=True) + pn
-        sc_b[...] = p
-        wait_bytes(v_b.at[l], wsem.at[l, 3], "w_v")
-        orow = lax.broadcasted_iota(jnp.int32, (G, D), 0)
-        for i in range(B // G):
-            b0 = i * G
-            pg = sc_b[b0:b0 + G, :].astype(BF16)
-            acc = jnp.zeros((G, D), F32)
-            for j in range(G):
-                t = jnp.dot(pg, v_b[l, b0 + j], preferred_element_type=F32)
-                acc = jnp.where(orow == j, t, acc)
-            of32[b0:b0 + G, :] = acc
-        o = of32[...] + pn * v.astype(F32)
+        den = d_b[...] * al + pn
+        o = of32[...] * al + pn * v.astype(F32)
         obuf[l, me_x] = (o / den).astype(BF16)
         for m in (2, 3, 1):
-            t = _partner(me_x, m)
+            t = px[m]
             remote(obuf.at[l, me_x], obuf.at[l, me_x], osend.at[l], orecv.at[l], me_y, t)
 
         for i in range(CH):
@@ -240,27 +267,33 @@
 
         wait_bytes(wout_b.at[l], wsem.at[l, 4], "w_wout")
 
-        def f_dot(c0):
-            f = jnp.concatenate([fbuf[l, c0 + i] for i in range(CH)], axis=1)
-            rows = pl.ds(pl.multiple_of(c0 * CW, CW), FH)
-            return jnp.dot(f, wout_b[l, rows, :], preferred_element_type=F32)
-
-        yacc[...] = f_dot(core * CH)
-        for i in range(CH):
+        def f_rows(c):
+            return pl.ds(pl.multiple_of(c * CW, CW), CW)
+
+        f = jnp.concatenate([fbuf[l, core * CH + i] for i in range(CH)], axis=1)
+        rows = pl.ds(pl.multiple_of(core * FH, FH), FH)
+        yacc[...] = jnp.dot(f, wout_b[l, rows, :], preferred_element_type=F32)
+        for i in range(CH - 1):
             wait_bytes(fbuf.at[l, i], crecv.at[l, i], "w_fg")
-        yacc[...] = yacc[...] + f_dot((1 - core) * CH)
+            c = (1 - core) * CH + i
+            yacc[...] = yacc[...] + jnp.dot(fbuf[l, c], wout_b[l, f_rows(c), :], preferred_element_type=F32)
         wait_bytes(wo_b.at[l], wsem.at[l, 5], "w_wo")
+        wait_bytes(fbuf.at[l, 0], crecv.at[l, CH - 1], "w_fg")
         wait_bytes(obuf.at[l, pl.ds(0, X - 1)], orecv.at[l], "w_og")
         og = jnp.concatenate([obuf[l, j] for j in range(X)], axis=1)
-        for m in masks[::2]:
-            z = lax.div(_partner(me_y, m), 2)
-            cols = pl.ds(pl.multiple_of(z * 2 * BLK, 2 * BLK), 2 * BLK)
-            acc = yacc[:, cols] + jnp.dot(og, wo_b[l, :, cols], preferred_element_type=F32)
-            ybuf[l, 2 * z] = acc[:, :BLK].astype(BF16)
-            ybuf[l, 2 * z + 1] = acc[:, BLK:].astype(BF16)
-            for n in (m, m - 1) if m > 1 else (m,):
-                t = _partner(me_y, n)
-                remote(ybuf.at[l, t], ry.at[l, n - 1], ysend.at[l], yrecv.at[l], t, me_x)
+        c = (1 - core) * CH + CH - 1
+        near = lax.div(me_y, Y // 2)
+        W = Y // 2 * BLK
+        for hz, ms in ((1 - near, masks[:Y // 2]), (near, masks[Y // 2:])):
+            cols = pl.ds(pl.multiple_of(hz * W, W), W)
+            acc = (yacc[:, cols] + jnp.dot(fbuf[l, c], wout_b[l, f_rows(c), cols], preferred_element_type=F32)
+                   + jnp.dot(og, wo_b[l, :, cols], preferred_element_type=F32))
+            for j in range(Y // 2):
+                ybuf[l, hz * (Y // 2) + j] = acc[:, j * BLK:(j + 1) * BLK].astype(BF16)
+            for m in ms:
+                remote(ybuf.at[l, py[m]], ry.at[l, m - 1], ysend.at[l], yrecv.at[l], py[m], me_x)
+        if l + 1 < L:
+            transpose_k(l + 1)
         wait_bytes(hbuf.at[l, pl.ds(0, Y - 1)], hsend.at[l])
         wait_bytes(ry.at[l], yrecv.at[l], "w_y")
         y = ybuf[l, me_y].astype(F32)
@@ -319,14 +352,14 @@
         V = pltpu.VMEM
         scratch = [
             V((L, E, 3 * HD), BF16), V((L, E, FL), BF16), V((L, HD, E), BF16), V((L, FL, E), BF16),
-            V((L, B, S, D), BF16), V((L, B, S, D), BF16),
+            V((L, B, S, D), BF16), V((L, B, S, D), BF16), V((B, D, S), BF16),
             V((B, BLK), BF16), V((L, Y, B, BLK), BF16), V((L, BLK), BF16), V((Y, L, BLK), BF16),
             V((1, B), jnp.int32), V((1, D), F32),
-            V((L, 1, D), F32), V((L, N - 1, 1, D), F32), V((B, Y * BLK), BF16),
+            V((L, 1, D), F32), V((L, N - Y, 1, D), F32), V((B, Y * BLK), BF16),
             V((B, D), F32), V((B, D), F32), V((B, D), F32),
             V((L, X, B, D), BF16), V((L, X, B, 2 * D), BF16),
             V((L, X - 1, B, D), BF16), V((L, X - 1, B, 2 * D), BF16),
-            V((B, D), BF16), V((B, S), F32), V((B, D), F32), V((L, X, B, D), BF16),
+            V((B, D), BF16), V((B, D), F32), V((B, D), F32), V((B, D), F32), V((L, X, B, D), BF16),
             V((L, CH, B, CW), BF16), V((L, CH, B, CW), BF16), V((CH, B, CW), F32),
             V((L, CH, B, CW), BF16), V((L, CH, B, CW), BF16), V((L, 2 * CH, B, CW), BF16),
             V((B, Y * BLK), F32), V((L, Y, B, BLK), BF16), V((L, Y - 1, B, BLK), BF16),

time: 50 us -> 47 us (0.940)
  Pallas kernels: 49.2 us -> 46.1 us
    pallas_call x1, Pallas kernels: 48.5 us -> 45.5 us  [body(): pl.pallas_call(functools.partial(_kernel, X, Y, float(BLK * N)), out_shap...]
where the time goes in v3:
time: 47 us; the launch traced here: 46.8 us
  Pallas kernels  46.1 us (98%)
  between operations  0.64 us (1%)
    pallas_call x1, Pallas kernels, body(): pl.pallas_call(functools.partial(_kernel, X, Y, float(BLK * N)), out_shap...  45.5 us

profile of v3, /device:TPU:0, one launch (start us, length us, event | category | flops | bytes accessed | tf_op | source)
XLA Modules:
  0.0 46.8 jit_solution(4429468372411943192)
XLA Ops:
  0.6 45.5 %decode_step.1 = (bf16[64,128]{1,0:T(8,128)(2,1)S(1)}, bf16[2,64,128]{2,1,0:T(8,128)(2,1)S(1)}, bf16[2,64,128]{2,1,0:T(8,128)(2,1)S(1)}) custom-call(bf16[64,128]{1,0:T(8,128)(2,1)} %h_ref.1, bf16[2,128]{1,0:T(2,128)(2,1)} %g_ref.1, s32[1,64]{1,0:T(1,128)} %bitcast.11, f32[1,128]{1,0:T(1,128)} %constant.2.clone.inv_ref, bf16[2,1024,512]{2,1,0:T(8,128)(2,1)} %wq.1, ...), custom_call_target="tpu_custom_call" | custom-call | tf_op jit(solution)/shard_map/decode_step/pallas_call | solution.py:373
  46.1 0.7 %finish.1 = (bf16[64,128]{1,0:T(8,128)(2,1)}, bf16[2,64,128]{2,1,0:T(8,128)(2,1)}, bf16[2,64,128]{2,1,0:T(8,128)(2,1)}) custom-call(bf16[64,128]{1,0:T(8,128)(2,1)S(1)} %get-tuple-element.9.h, bf16[2,64,128]{2,1,0:T(8,128)(2,1)S(1)} %get-tuple-element.10.k, bf16[2,64,128]{2,1,0:T(8,128)(2,1)S(1)} %get-tuple-element.11.v), custom_call_target="tpu_custom_call" | custom-call | tf_op jit(solution)/shard_map/finish/pallas_call | solution.py:383

commit v4 on v3

v4 whole, which is shorter than its diff:
```python
import functools
import math

import numpy as np

import jax
import jax.numpy as jnp
from jax import lax
from jax.experimental import pallas as pl
from jax.experimental.pallas import tpu as pltpu
from jax.sharding import PartitionSpec as P

EPS = 1e-6
MESH = pl.DeviceIdType.MESH
F32 = jnp.float32
BF16 = jnp.bfloat16
QUARTERS = ((0, 2), (2, 1), (3, 1))
NC = len(QUARTERS)


def _gelu(x):
    return 0.5 * x * (1.0 + jnp.tanh(math.sqrt(2.0 / math.pi) * (x + 0.044715 * (x * x * x))))


def _partner(i, mask):
    bit = 1
    t = i
    while bit <= mask:
        if mask & bit:
            t = t + bit * (1 - 2 * lax.rem(lax.div(i, bit), 2))
        bit *= 2
    return t


def _kernel(X, Y, e_total, h_ref, g_ref, lens_ref, inv_ref, wq, wk, wv, w_in, wo, w_out, kc, vc,
            h_out, k_out, v_out,
            wqkv_b, win_b, wo_b, wout_b, k_b, v_b, kt_b,
            hx, hbuf0, hbuf, lens_b, inv_b, ssown, ssbuf, xs, cos_b, sin_b, lenb,
            pq, pk, pv, rq, rv, rks, kx, rkx, q_b, m_b, d_b, of32, obuf,
            fsib, fsibr, fown, fcross, fcrossr, fbuf, yacc, ybuf, ry,
            isem, wsem, sent, hrecv, srecv, qrecv, arecv, brecv, crecv, orecv, ysend, yrecv):
    me_y = lax.axis_index("yz")
    me_x = lax.axis_index("x")
    N = X * Y
    L = wqkv_b.shape[0]
    B, BLK = h_ref.shape
    S, D = kc.shape[2], kc.shape[3]
    HD = wq.shape[2]
    FL = w_in.shape[2]
    FH = FL // 2
    HW = FH // 2
    CW = FH // 4
    half = D // 2
    core = lax.rem(me_x, 2)
    py = [_partner(me_y, m) for m in range(Y)]
    px = [_partner(me_x, m) for m in range(X)]
    sib, cross = px[1], px[2]
    masks = list(range(Y - 1, 0, -1))
    near = lax.div(me_y, Y // 2)
    total = [0]

    barrier = pltpu.get_barrier_semaphore()
    for m in range(Y - 1, -1, -1):
        for n in range(X - 1, -1, -1):
            if m or n:
                pl.semaphore_signal(barrier, inc=1, device_id=(py[m], px[n]), device_id_type=MESH)

    def remote(src, dst, recv, y, x, send=None):
        if send is None:
            total[0] += math.prod(src.shape) * np.dtype(src.dtype).itemsize
        pltpu.make_async_remote_copy(src, dst, sent if send is None else send, recv,
                                     device_id=(y, x), device_id_type=MESH).start()

    def wait_bytes(ref, sem, name="wait"):
        with jax.named_scope(name):
            pltpu.make_async_copy(ref, ref, sem).wait()

    inputs = [pltpu.make_async_copy(s, d, isem) for s, d in (
        (h_ref, hx.at[pl.ds(0, B)]), (g_ref, hx.at[pl.ds(B, L)]), (lens_ref, lens_b), (inv_ref, inv_b))]
    for c in inputs:
        c.start()

    def load(w, b, l, i, parts=4):
        n = w.shape[1] // parts
        for j in range(parts):
            pltpu.make_async_copy(w.at[l, pl.ds(j * n, n)], b.at[l, pl.ds(j * n, n)], wsem.at[i]).start()

    def load_qkv(l, i):
        for j, w in enumerate((wq, wk, wv)):
            pltpu.make_async_copy(w.at[l], wqkv_b.at[l, :, pl.ds(j * HD, HD)], wsem.at[i]).start()

    def transpose_k(l):
        wait_bytes(k_b.at[l], wsem.at[3 * l], "w_k")

        def step(i, carry):
            for j in range(8):
                kt_b[i * 8 + j] = k_b[l, i * 8 + j].T
            return carry

        with jax.named_scope("kt"):
            lax.fori_loop(0, B // 8, step, 0)

    for c in inputs:
        c.wait()
    load(kc, k_b, 0, 0)
    load_qkv(0, 1)
    load(w_in, win_b, 0, 1)
    load(vc, v_b, 0, 2)
    load(w_out, wout_b, 0, 2)
    load(wo, wo_b, 0, 2, 1)
    for l in range(1, L):
        load(kc, k_b, l, 3)
        load_qkv(l, 4)
        load(w_in, win_b, l, 4)
        load(vc, v_b, l, 4)
        load(w_out, wout_b, l, 4)
        load(wo, wo_b, l, 4, 1)

    row = lax.broadcasted_iota(jnp.int32, (B, D), 0)
    lane = lax.broadcasted_iota(jnp.int32, (B, D), 1)

    def column(r):
        return jnp.sum(jnp.where(row == lane, jnp.broadcast_to(r, (B, D)), 0.0), axis=1, keepdims=True)

    def as_row(c):
        return jnp.sum(jnp.where(row == lane, jnp.broadcast_to(c, (B, D)), 0.0), axis=0, keepdims=True)

    lens_row = jnp.concatenate([lens_b[...].astype(F32), jnp.zeros((1, D - B), F32)], axis=1)
    lens_col = column(lens_row)
    lenb[...] = jnp.broadcast_to(lens_col, (B, D))
    ang = lens_col * inv_b[...]
    cos_b[...] = jnp.cos(ang)
    sn = jnp.sin(ang)
    sin_b[...] = jnp.where(lane < half, -sn, sn)

    def rope(t):
        tf = t.astype(F32)
        return (tf * cos_b[...] + pltpu.roll(tf, half, 1) * sin_b[...]).astype(BF16)

    def send_ss(l, hn):
        hf = hn.astype(F32)
        ssown[l] = as_row(jnp.sum(hf * hf, axis=1, keepdims=True))

    def exchange_h(l, src, dst):
        for m in range(Y - 1, -1, -1):
            for n in range(X - 1, 0, -1):
                remote(ssown.at[l], ssbuf.at[l, m * (X - 1) + n - 1], srecv, py[m], px[n])
        for m in masks:
            remote(src, dst.at[me_y], hrecv, py[m], me_x)

    send_ss(0, hx[0:B])
    hbuf0[me_y] = hx[...]

    with jax.named_scope("w_bar"):
        pl.semaphore_wait(barrier, N - 1)
    exchange_h(0, hx, hbuf0)
    transpose_k(0)

    for l in range(L):
        last = l == L - 1
        hall = hbuf if l else hbuf0
        wait_bytes(hall.at[pl.ds(0, Y - 1)], hrecv, "w_h")
        wait_bytes(ssbuf.at[l], srecv, "w_ss")
        row_ss = jnp.zeros((B, BLK), F32)
        for j in range(Y):
            hf = hall[j, 0:B].astype(F32)
            row_ss = row_ss + hf * hf
        tot = jnp.sum(row_ss, axis=1, keepdims=True) + column(jnp.sum(ssbuf[l], axis=0))
        r = lax.rsqrt(tot / e_total + EPS)
        for j in range(Y):
            gl = hbuf0[j, B + l:B + l + 1].astype(F32)
            xs[:, j * BLK:(j + 1) * BLK] = (hall[j, 0:B].astype(F32) * r * gl).astype(BF16)

        if l == 0:
            wait_bytes(wqkv_b.at[l], wsem.at[1], "w_wqkv")
            wait_bytes(win_b.at[l], wsem.at[1], "w_win")
        else:
            for b in (wqkv_b, win_b, v_b, wout_b, wo_b):
                wait_bytes(b.at[l], wsem.at[4], "w_w1")

        def part(i, dst):
            p = jnp.dot(xs[...], wqkv_b[l, :, i * HD:(i + 1) * HD], preferred_element_type=F32).astype(BF16)
            for j in range(X):
                dst[l, j] = p[:, j * D:(j + 1) * D]

        part(0, pq)
        for m in (2, 3, 1):
            remote(pq.at[l, px[m]], rq.at[l, m - 1], qrecv.at[0], me_y, px[m])
        part(1, pk)
        for i, t in enumerate((px[3], sib)):
            remote(pk.at[l, t], rks.at[l, i], qrecv.at[1], me_y, sib)
        part(2, pv)
        for m in (2, 3, 1):
            remote(pv.at[l, px[m]], rv.at[l, m - 1], qrecv.at[2], me_y, px[m])


        def f_part(c, i):
            cols = pl.ds(pl.multiple_of(c * FH + i * HW, HW), HW)
            return jnp.dot(xs[...], win_b[l, :, cols], preferred_element_type=F32)

        def f_sib(i):
            fsib[l, i] = f_part(1 - core, i).astype(BF16)
            remote(fsib.at[l, i], fsibr.at[l, i], arecv.at[i], me_y, sib)

        def f_add(i):
            wait_bytes(fsibr.at[l, i], arecv.at[i], "w_fs")
            s = fown[i] + fsibr[l, i].astype(F32)
            fown[i] = s
            for j in range(2):
                fcross[l, 2 * i + j] = s[:, j * CW:(j + 1) * CW].astype(BF16)
            for c, (q0, nq) in enumerate(QUARTERS):
                if q0 // 2 == i:
                    qs = pl.ds(q0, nq)
                    remote(fcross.at[l, qs], fcrossr.at[l, qs], brecv.at[c], me_y, cross)

        f_sib(0)
        fown[0] = f_part(core, 0)
        wait_bytes(rks.at[l], qrecv.at[1], "w_ks")
        kx[l] = (pk[l, cross].astype(F32) + rks[l, 0].astype(F32)).astype(BF16)
        remote(kx.at[l], rkx.at[l], qrecv.at[3], me_y, cross)
        f_sib(1)
        f_add(0)
        fown[1] = f_part(core, 1)
        f_add(1)

        scale = D ** -0.5
        if l == 0:
            for b in (v_b, wout_b, wo_b):
                wait_bytes(b.at[l], wsem.at[2], "w_v")
        wait_bytes(rq.at[l], qrecv.at[0], "w_q")
        s = pq[l, me_x].astype(F32)
        for d in range(X - 1):
            s = s + rq[l, d].astype(F32)
        q = rope(s.astype(BF16))
        q_b[...] = q
        G = 16
        grow = lax.broadcasted_iota(jnp.int32, (G, S), 0)
        orow = lax.broadcasted_iota(jnp.int32, (G, D), 0)
        pos = lax.broadcasted_iota(jnp.int32, (G, S), 1).astype(F32)

        def scores(i):
            b0 = i * G
            qg = q_b[b0:b0 + G, :]
            acc = jnp.zeros((G, S), F32)
            for j in range(G):
                acc = jnp.where(grow == j, jnp.dot(qg, kt_b[b0 + j], preferred_element_type=F32), acc)
            ln = lenb[b0:b0 + G, :]
            sc = jnp.where(pos < jnp.concatenate([ln] * (S // D), axis=1), acc * scale, -jnp.inf)
            m = jnp.max(sc, axis=1, keepdims=True)
            p = jnp.exp(sc - m)
            m_b[b0:b0 + G, :] = jnp.broadcast_to(m, (G, D))
            d_b[b0:b0 + G, :] = jnp.broadcast_to(jnp.sum(p, axis=1, keepdims=True), (G, D))
            return p.astype(BF16)

        def values(i, p):
            b0 = i * G
            acc = jnp.zeros((G, D), F32)
            for j in range(G):
                acc = jnp.where(orow == j, jnp.dot(p, v_b[l, b0 + j], preferred_element_type=F32), acc)
            of32[b0:b0 + G, :] = acc

        with jax.named_scope("attn"):
            prev = scores(0)
            for i in range(1, B // G):
                cur = scores(i)
                values(i - 1, prev)
                prev = cur
            values(B // G - 1, prev)

        wait_bytes(rv.at[l], qrecv.at[2], "w_nv")
        wait_bytes(rkx.at[l], qrecv.at[3], "w_nk")
        s = pv[l, me_x].astype(F32)
        for d in range(X - 1):
            s = s + rv[l, d].astype(F32)
        v = s.astype(BF16)
        k = rope((pk[l, me_x].astype(F32) + rks[l, 1].astype(F32) + rkx[l].astype(F32)).astype(BF16))
        sn = jnp.sum(q_b[...].astype(F32) * k.astype(F32), axis=1, keepdims=True) * scale
        m = jnp.maximum(m_b[...], sn)
        al = jnp.exp(m_b[...] - m)
        pn = jnp.exp(sn - m)
        den = d_b[...] * al + pn
        o = of32[...] * al + pn * v.astype(F32)
        obuf[l, me_x] = (o / den).astype(BF16)
        for m in (2, 3, 1):
            remote(obuf.at[l, me_x], obuf.at[l, me_x], orecv, me_y, px[m])
        k_out[l] = k
        v_out[l] = v

        def f_dot(q0, nq, cols):
            f = jnp.concatenate([fbuf[l, q0 + i] for i in range(nq)], axis=1)
            rows = pl.ds(pl.multiple_of(q0 * CW, CW), nq * CW)
            return jnp.dot(f, wout_b[l, rows, cols], preferred_element_type=F32)

        mine, other = core * 4, (1 - core) * 4
        everything = slice(None)
        for c, (q0, nq) in enumerate(QUARTERS):
            wait_bytes(fcrossr.at[l, pl.ds(q0, nq)], brecv.at[c], "w_fc")
            for i in range(q0, q0 + nq):
                s = fown[i // 2, :, (i % 2) * CW:(i % 2 + 1) * CW] + fcrossr[l, i].astype(F32)
                fbuf[l, mine + i] = _gelu(s.astype(BF16).astype(F32)).astype(BF16)
            qs = pl.ds(mine + q0, nq)
            remote(fbuf.at[l, qs], fbuf.at[l, qs], crecv.at[c], me_y, sib)
            if c == 0:
                yacc[...] = f_dot(mine + q0, nq, everything)
            elif c == 1:
                yacc[...] = yacc[...] + f_dot(mine + q0, nq, everything)
            else:
                p0, np_ = QUARTERS[0]
                wait_bytes(fbuf.at[l, pl.ds(p0, np_)], crecv.at[0], "w_fg")
                yacc[...] = yacc[...] + (f_dot(mine + q0, nq, everything) + f_dot(other + p0, np_, everything))
        p0, np_ = QUARTERS[1]
        wait_bytes(fbuf.at[l, pl.ds(p0, np_)], crecv.at[1], "w_fg")
        wait_bytes(obuf.at[l, pl.ds(0, X - 1)], orecv, "w_og")
        og = jnp.concatenate([obuf[l, j] for j in range(X)], axis=1)
        yacc[...] = yacc[...] + (f_dot(other + p0, np_, everything)
                                 + jnp.dot(og, wo_b[l], preferred_element_type=F32))
        p0, np_ = QUARTERS[2]
        wait_bytes(fbuf.at[l, pl.ds(p0, np_)], crecv.at[2], "w_fg")
        W = Y // 2 * BLK
        for hz, ms in ((1 - near, masks[:Y // 2]), (near, masks[Y // 2:])):
            cols = pl.ds(pl.multiple_of(hz * W, W), W)
            acc = yacc[:, cols] + f_dot(other + p0, np_, cols)
            for j in range(Y // 2):
                ybuf[l, hz * (Y // 2) + j] = acc[:, j * BLK:(j + 1) * BLK].astype(BF16)
            for m in ms:
                remote(ybuf.at[l, py[m]], ry.at[l, m - 1], yrecv, py[m], me_x, ysend if last else None)
        if last:
            n = total[0]
            big = S * D * 2
            wait_bytes(k_b.at[0, pl.ds(0, n // big)], sent)
            if n % big:
                wait_bytes(k_b.at[0, 0, pl.ds(0, n % big // (2 * D))], sent)
            wait_bytes(ry.at[l], ysend)
        else:
            transpose_k(l + 1)
        wait_bytes(ry.at[l], yrecv, "w_y")
        y = ybuf[l, me_y].astype(F32)
        for d in range(Y - 1):
            y = y + ry[l, d].astype(F32)
        hn = (hall[me_y, 0:B].astype(F32) + y.astype(BF16).astype(F32)).astype(BF16)
        if last:
            h_out[...] = hn
        else:
            send_ss(l + 1, hn)
            hbuf[me_y] = hn
            exchange_h(l + 1, hbuf.at[me_y], hbuf)


def _finish(h, k, v, h_out, k_out, v_out, sem):
    copies = [pltpu.make_async_copy(a, b, sem.at[i]) for i, (a, b) in enumerate(((k, k_out), (v, v_out), (h, h_out)))]
    for c in copies:
        c.start()
    for c in copies:
        c.wait()


def solution(mesh):
    X = mesh.shape['x']
    Y = mesh.shape['yz']
    act = P(None, ('x', 'yz'))
    w_first = P(None, 'x', 'yz')
    w_second = P(None, 'yz', 'x')
    cache = P(None, None, ('yz', 'x'), None, None)
    new = P(None, None, ('yz', 'x'), None)

    def body(h, g, wq, wk, wv, w_in, wo, w_out, kc, vc, lens):
        B, BLK = h.shape
        L, E, HD = wq.shape
        FL = w_in.shape[2]
        S, D = kc.shape[3], kc.shape[4]
        half = D // 2
        CW = FL // 8
        kc = kc.reshape(L, B, S, D)
        vc = vc.reshape(L, B, S, D)
        i = np.arange(half, dtype=np.float32)
        inv = np.power(np.float32(10000.0), -i / np.float32(half)).astype(np.float32)
        inv = jnp.asarray(np.concatenate([inv, inv])[None])
        vm = pl.BlockSpec(memory_space=pltpu.VMEM)
        hbm = pl.BlockSpec(memory_space=pl.ANY)
        far = pl.BlockSpec(memory_space=pltpu.HBM)
        N = X * Y
        dma = pltpu.SemaphoreType.DMA
        V = pltpu.VMEM
        scratch = [
            V((L, E, 3 * HD), BF16), V((L, E, FL), BF16), V((L, HD, E), BF16), V((L, FL, E), BF16),
            V((L, B, S, D), BF16), V((L, B, S, D), BF16), V((B, D, S), BF16),
            V((B + 8, BLK), BF16), V((Y, B + 8, BLK), BF16), V((Y, B, BLK), BF16),
            V((1, B), jnp.int32), V((1, D), F32),
            V((L, 1, D), F32), V((L, N - Y, 1, D), F32), V((B, Y * BLK), BF16),
            V((B, D), F32), V((B, D), F32), V((B, D), F32),
            V((L, X, B, D), BF16), V((L, X, B, D), BF16), V((L, X, B, D), BF16),
            V((L, X - 1, B, D), BF16), V((L, X - 1, B, D), BF16), V((L, 2, B, D), BF16),
            V((L, B, D), BF16), V((L, B, D), BF16),
            V((B, D), BF16), V((B, D), F32), V((B, D), F32), V((B, D), F32), V((L, X, B, D), BF16),
            V((L, 2, B, 2 * CW), BF16), V((L, 2, B, 2 * CW), BF16), V((2, B, 2 * CW), F32),
            V((L, 4, B, CW), BF16), V((L, 4, B, CW), BF16), V((L, 8, B, CW), BF16),
            V((B, Y * BLK), F32), V((L, Y, B, BLK), BF16), V((L, Y - 1, B, BLK), BF16),
            dma, dma((5,)), dma, dma, dma, dma((4,)), dma((2,)), dma((NC,)), dma((NC,)), dma, dma, dma,
        ]
        shapes = (jax.ShapeDtypeStruct((B, BLK), BF16),
                  jax.ShapeDtypeStruct((L, B, D), BF16),
                  jax.ShapeDtypeStruct((L, B, D), BF16))
        outs = pl.pallas_call(
            functools.partial(_kernel, X, Y, float(BLK * N)),
            out_shape=tuple(V(t.shape, t.dtype) for t in shapes),
            in_specs=[hbm] * 12,
            out_specs=(vm, vm, vm),
            scratch_shapes=scratch,
            compiler_params=pltpu.CompilerParams(
                collective_id=0, has_side_effects=True, vmem_limit_bytes=56 * 1024 * 1024),
            name="decode_step",
        )(h, g, lens.reshape(1, B), inv, wq, wk, wv, w_in, wo, w_out, kc, vc)
        h_new, k_new, v_new = pl.pallas_call(
            _finish, out_shape=shapes, in_specs=[vm] * 3, out_specs=(far, far, far), name="finish",
            scratch_shapes=[dma((3,))],
        )(*[pltpu.with_memory_space_constraint(t, pltpu.VMEM) for t in outs])
        return h_new, k_new.reshape(L, B, 1, D), v_new.reshape(L, B, 1, D)

    return jax.shard_map(
        body, mesh=mesh,
        in_specs=(act, act, w_first, w_first, w_first, w_first, w_second, w_second, cache, cache, P(None)),
        out_specs=(act, new, new), check_vma=False)
```

time: 47 us -> 46.1 us (0.981)
  Pallas kernels: 46.1 us -> 45.3 us
    pallas_call x1, Pallas kernels: 45.5 us -> 44.6 us  [body(): pl.pallas_call(functools.partial(_kernel, X, Y, float(BLK * N)), out_shap...]
where the time goes in v4:
time: 46.1 us; the launch traced here: 45.9 us
  Pallas kernels  45.3 us (98%)
  between operations  0.64 us (1%)
    pallas_call x1, Pallas kernels, body(): pl.pallas_call(functools.partial(_kernel, X, Y, float(BLK * N)), out_shap...  44.6 us

profile of v4, /device:TPU:0, one launch (start us, length us, event | category | flops | bytes accessed | tf_op | source)
XLA Modules:
  0.0 45.9 jit_solution(6542904977973233940)
XLA Ops:
  0.6 44.6 %decode_step.1 = (bf16[64,128]{1,0:T(8,128)(2,1)S(1)}, bf16[2,64,128]{2,1,0:T(8,128)(2,1)S(1)}, bf16[2,64,128]{2,1,0:T(8,128)(2,1)S(1)}) custom-call(bf16[64,128]{1,0:T(8,128)(2,1)} %h_ref.1, bf16[2,128]{1,0:T(2,128)(2,1)} %g_ref.1, s32[1,64]{1,0:T(1,128)} %bitcast.11, f32[1,128]{1,0:T(1,128)} %constant.2.clone.inv_ref, bf16[2,1024,512]{2,1,0:T(8,128)(2,1)} %wq.1, ...), custom_call_target="tpu_custom_call" | custom-call | tf_op jit(solution)/shard_map/decode_step/pallas_call | solution.py:403
  45.2 0.7 %finish.1 = (bf16[64,128]{1,0:T(8,128)(2,1)}, bf16[2,64,128]{2,1,0:T(8,128)(2,1)}, bf16[2,64,128]{2,1,0:T(8,128)(2,1)}) custom-call(bf16[64,128]{1,0:T(8,128)(2,1)S(1)} %get-tuple-element.9.h, bf16[2,64,128]{2,1,0:T(8,128)(2,1)S(1)} %get-tuple-element.10.k, bf16[2,64,128]{2,1,0:T(8,128)(2,1)S(1)} %get-tuple-element.11.v), custom_call_target="tpu_custom_call" | custom-call | tf_op jit(solution)/shard_map/finish/pallas_call | solution.py:413

commit v5 on v4

--- a/solution.py
+++ b/solution.py
@@ -16,6 +16,7 @@
 BF16 = jnp.bfloat16
 QUARTERS = ((0, 2), (2, 1), (3, 1))
 NC = len(QUARTERS)
+UP, DOWN = 2.0 ** 18, 2.0 ** -18
 
 
 def _gelu(x):
@@ -32,16 +33,15 @@
     return t
 
 
-def _kernel(X, Y, e_total, h_ref, g_ref, lens_ref, inv_ref, wq, wk, wv, w_in, wo, w_out, kc, vc,
+def _kernel(X, Y, h_ref, g_ref, lens_ref, inv_ref, wq, wk, wv, w_in, wo, w_out, kc, vc,
             h_out, k_out, v_out,
             wqkv_b, win_b, wo_b, wout_b, k_b, v_b, kt_b,
-            hx, hbuf0, hbuf, lens_b, inv_b, ssown, ssbuf, xs, cos_b, sin_b, lenb,
+            hx, hbuf0, hbuf, lens_b, inv_b, mown, mrow, xs, cos_b, sin_b, lenb,
             pq, pk, pv, rq, rv, rks, kx, rkx, q_b, m_b, d_b, of32, obuf,
             fsib, fsibr, fown, fcross, fcrossr, fbuf, yacc, ybuf, ry,
-            isem, wsem, sent, hrecv, srecv, qrecv, arecv, brecv, crecv, orecv, ysend, yrecv):
+            isem, wsem, sent, hrecv, mrecv, qrecv, arecv, brecv, crecv, orecv, ysend, yrecv):
     me_y = lax.axis_index("yz")
     me_x = lax.axis_index("x")
-    N = X * Y
     L = wqkv_b.shape[0]
     B, BLK = h_ref.shape
     S, D = kc.shape[2], kc.shape[3]
@@ -60,10 +60,10 @@
     total = [0]
 
     barrier = pltpu.get_barrier_semaphore()
-    for m in range(Y - 1, -1, -1):
-        for n in range(X - 1, -1, -1):
-            if m or n:
-                pl.semaphore_signal(barrier, inc=1, device_id=(py[m], px[n]), device_id_type=MESH)
+    for m in masks:
+        pl.semaphore_signal(barrier, inc=1, device_id=(py[m], me_x), device_id_type=MESH)
+    for n in range(X - 1, 0, -1):
+        pl.semaphore_signal(barrier, inc=1, device_id=(me_y, px[n]), device_id_type=MESH)
 
     def remote(src, dst, recv, y, x, send=None):
         if send is None:
@@ -137,39 +137,42 @@
         tf = t.astype(F32)
         return (tf * cos_b[...] + pltpu.roll(tf, half, 1) * sin_b[...]).astype(BF16)
 
-    def send_ss(l, hn):
-        hf = hn.astype(F32)
-        ssown[l] = as_row(jnp.sum(hf * hf, axis=1, keepdims=True))
-
-    def exchange_h(l, src, dst):
-        for m in range(Y - 1, -1, -1):
-            for n in range(X - 1, 0, -1):
-                remote(ssown.at[l], ssbuf.at[l, m * (X - 1) + n - 1], srecv, py[m], px[n])
+    def exchange_h(src, dst):
         for m in masks:
             remote(src, dst.at[me_y], hrecv, py[m], me_x)
 
-    send_ss(0, hx[0:B])
+    def rms(ss, n):
+        return jnp.minimum(jnp.sqrt(ss / n + EPS), 1e38)
+
+    lane1 = lax.broadcasted_iota(jnp.int32, (1, D), 1)
+    NX = Y * BLK
+
     hbuf0[me_y] = hx[...]
 
     with jax.named_scope("w_bar"):
-        pl.semaphore_wait(barrier, N - 1)
-    exchange_h(0, hx, hbuf0)
+        pl.semaphore_wait(barrier, X + Y - 2)
+    exchange_h(hx, hbuf0)
     transpose_k(0)
 
     for l in range(L):
         last = l == L - 1
         hall = hbuf if l else hbuf0
         wait_bytes(hall.at[pl.ds(0, Y - 1)], hrecv, "w_h")
-        wait_bytes(ssbuf.at[l], srecv, "w_ss")
         row_ss = jnp.zeros((B, BLK), F32)
+        gmax = jnp.zeros((1, BLK), F32)
         for j in range(Y):
             hf = hall[j, 0:B].astype(F32)
             row_ss = row_ss + hf * hf
-        tot = jnp.sum(row_ss, axis=1, keepdims=True) + column(jnp.sum(ssbuf[l], axis=0))
-        r = lax.rsqrt(tot / e_total + EPS)
+            gmax = jnp.maximum(gmax, jnp.abs(hbuf0[j, B + l:B + l + 1].astype(F32)))
+        ss = jnp.sum(row_ss, axis=1, keepdims=True)
+        G = jnp.maximum(jnp.max(gmax, axis=1, keepdims=True), 2.0 ** -100)
+        mown[l] = jnp.where(lane1 == B, G, as_row(ss))
+        for m in (1, 2, 3):
+            remote(mown.at[l], mrow.at[l, m - 1], mrecv.at[0 if m == 1 else 1], me_y, px[m])
+        sx = lax.rsqrt(ss / NX + EPS)
         for j in range(Y):
-            gl = hbuf0[j, B + l:B + l + 1].astype(F32)
-            xs[:, j * BLK:(j + 1) * BLK] = (hall[j, 0:B].astype(F32) * r * gl).astype(BF16)
+            gl = (hbuf0[j, B + l:B + l + 1].astype(F32) / G) * DOWN
+            xs[:, j * BLK:(j + 1) * BLK] = (hall[j, 0:B].astype(F32) * sx * gl).astype(BF16)
 
         if l == 0:
             wait_bytes(wqkv_b.at[l], wsem.at[1], "w_wqkv")
@@ -204,19 +207,25 @@
 
         def f_add(i):
             wait_bytes(fsibr.at[l, i], arecv.at[i], "w_fs")
-            s = fown[i] + fsibr[l, i].astype(F32)
+            s = fown[i] * w_own + fsibr[l, i].astype(F32) * w_sib
             fown[i] = s
             for j in range(2):
                 fcross[l, 2 * i + j] = s[:, j * CW:(j + 1) * CW].astype(BF16)
             for c, (q0, nq) in enumerate(QUARTERS):
                 if q0 // 2 == i:
                     qs = pl.ds(q0, nq)
-                    remote(fcross.at[l, qs], fcrossr.at[l, qs], brecv.at[c], me_y, cross)
+                    remote(fcross.at[l, qs], fcrossr.at[l, qs], brecv.at[l, c], me_y, cross)
 
         f_sib(0)
         fown[0] = f_part(core, 0)
+        wait_bytes(mrow.at[l, 0], mrecv.at[0], "w_ms")
+        ss1, G1 = column(mrow[l, 0]), mrow[l, 0, :, B:B + 1]
+        ssc, Gc = ss + ss1, jnp.maximum(G, G1)
+        sc_ = lax.rsqrt(ssc / (2 * NX) + EPS)
+        w_own = sc_ * rms(ss, NX) * (G / Gc)
+        w_sib = sc_ * rms(ss1, NX) * (G1 / Gc)
         wait_bytes(rks.at[l], qrecv.at[1], "w_ks")
-        kx[l] = (pk[l, cross].astype(F32) + rks[l, 0].astype(F32)).astype(BF16)
+        kx[l] = (pk[l, cross].astype(F32) * w_own + rks[l, 0].astype(F32) * w_sib).astype(BF16)
         remote(kx.at[l], rkx.at[l], qrecv.at[3], me_y, cross)
         f_sib(1)
         f_add(0)
@@ -227,53 +236,64 @@
         if l == 0:
             for b in (v_b, wout_b, wo_b):
                 wait_bytes(b.at[l], wsem.at[2], "w_v")
+        wait_bytes(mrow.at[l, pl.ds(1, 2)], mrecv.at[1], "w_m")
+        ss2, G2 = column(mrow[l, 1]), mrow[l, 1, :, B:B + 1]
+        ss3, G3 = column(mrow[l, 2]), mrow[l, 2, :, B:B + 1]
+        ssd, Gd = ss2 + ss3, jnp.maximum(G2, G3)
+        r = lax.rsqrt((ssc + ssd) / (4 * NX) + EPS)
+        rows4 = [(r * rms(a, NX), b) for a, b in ((ss, G), (ss1, G1), (ss2, G2), (ss3, G3))]
+        fc, fd = r * rms(ssc, 2 * NX), r * rms(ssd, 2 * NX)
+
+        def joined(p, got):
+            s = (p.astype(F32) * rows4[0][0]) * rows4[0][1]
+            for d in range(X - 1):
+                s = s + (got[d].astype(F32) * rows4[d + 1][0]) * rows4[d + 1][1]
+            return (s * UP).astype(BF16)
+
+        def chips(mine, theirs):
+            return (((mine * fc) * Gc + (theirs * fd) * Gd) * UP).astype(BF16)
+
         wait_bytes(rq.at[l], qrecv.at[0], "w_q")
-        s = pq[l, me_x].astype(F32)
-        for d in range(X - 1):
-            s = s + rq[l, d].astype(F32)
-        q = rope(s.astype(BF16))
+        q = rope(joined(pq[l, me_x], rq[l]))
         q_b[...] = q
-        G = 16
-        grow = lax.broadcasted_iota(jnp.int32, (G, S), 0)
-        orow = lax.broadcasted_iota(jnp.int32, (G, D), 0)
-        pos = lax.broadcasted_iota(jnp.int32, (G, S), 1).astype(F32)
+        GB = 16
+        grow = lax.broadcasted_iota(jnp.int32, (GB, S), 0)
+        orow = lax.broadcasted_iota(jnp.int32, (GB, D), 0)
+        pos = lax.broadcasted_iota(jnp.int32, (GB, S), 1).astype(F32)
 
         def scores(i):
-            b0 = i * G
-            qg = q_b[b0:b0 + G, :]
-            acc = jnp.zeros((G, S), F32)
-            for j in range(G):
+            b0 = i * GB
+            qg = q_b[b0:b0 + GB, :]
+            acc = jnp.zeros((GB, S), F32)
+            for j in range(GB):
                 acc = jnp.where(grow == j, jnp.dot(qg, kt_b[b0 + j], preferred_element_type=F32), acc)
-            ln = lenb[b0:b0 + G, :]
+            ln = lenb[b0:b0 + GB, :]
             sc = jnp.where(pos < jnp.concatenate([ln] * (S // D), axis=1), acc * scale, -jnp.inf)
             m = jnp.max(sc, axis=1, keepdims=True)
             p = jnp.exp(sc - m)
-            m_b[b0:b0 + G, :] = jnp.broadcast_to(m, (G, D))
-            d_b[b0:b0 + G, :] = jnp.broadcast_to(jnp.sum(p, axis=1, keepdims=True), (G, D))
+            m_b[b0:b0 + GB, :] = jnp.broadcast_to(m, (GB, D))
+            d_b[b0:b0 + GB, :] = jnp.broadcast_to(jnp.sum(p, axis=1, keepdims=True), (GB, D))
             return p.astype(BF16)
 
         def values(i, p):
-            b0 = i * G
-            acc = jnp.zeros((G, D), F32)
-            for j in range(G):
+            b0 = i * GB
+            acc = jnp.zeros((GB, D), F32)
+            for j in range(GB):
                 acc = jnp.where(orow == j, jnp.dot(p, v_b[l, b0 + j], preferred_element_type=F32), acc)
-            of32[b0:b0 + G, :] = acc
+            of32[b0:b0 + GB, :] = acc
 
         with jax.named_scope("attn"):
             prev = scores(0)
-            for i in range(1, B // G):
+            for i in range(1, B // GB):
                 cur = scores(i)
                 values(i - 1, prev)
                 prev = cur
-            values(B // G - 1, prev)
+            values(B // GB - 1, prev)
 
         wait_bytes(rv.at[l], qrecv.at[2], "w_nv")
         wait_bytes(rkx.at[l], qrecv.at[3], "w_nk")
-        s = pv[l, me_x].astype(F32)
-        for d in range(X - 1):
-            s = s + rv[l, d].astype(F32)
-        v = s.astype(BF16)
-        k = rope((pk[l, me_x].astype(F32) + rks[l, 1].astype(F32) + rkx[l].astype(F32)).astype(BF16))
+        v = joined(pv[l, me_x], rv[l])
+        k = rope(chips(pk[l, me_x].astype(F32) * w_own + rks[l, 1].astype(F32) * w_sib, rkx[l].astype(F32)))
         sn = jnp.sum(q_b[...].astype(F32) * k.astype(F32), axis=1, keepdims=True) * scale
         m = jnp.maximum(m_b[...], sn)
         al = jnp.exp(m_b[...] - m)
@@ -294,10 +314,10 @@
         mine, other = core * 4, (1 - core) * 4
         everything = slice(None)
         for c, (q0, nq) in enumerate(QUARTERS):
-            wait_bytes(fcrossr.at[l, pl.ds(q0, nq)], brecv.at[c], "w_fc")
+            wait_bytes(fcrossr.at[l, pl.ds(q0, nq)], brecv.at[l, c], "w_fc")
             for i in range(q0, q0 + nq):
-                s = fown[i // 2, :, (i % 2) * CW:(i % 2 + 1) * CW] + fcrossr[l, i].astype(F32)
-                fbuf[l, mine + i] = _gelu(s.astype(BF16).astype(F32)).astype(BF16)
+                u = chips(fown[i // 2, :, (i % 2) * CW:(i % 2 + 1) * CW], fcrossr[l, i].astype(F32))
+                fbuf[l, mine + i] = _gelu(u.astype(F32)).astype(BF16)
             qs = pl.ds(mine + q0, nq)
             remote(fbuf.at[l, qs], fbuf.at[l, qs], crecv.at[c], me_y, sib)
             if c == 0:
@@ -341,9 +361,8 @@
         if last:
             h_out[...] = hn
         else:
-            send_ss(l + 1, hn)
             hbuf[me_y] = hn
-            exchange_h(l + 1, hbuf.at[me_y], hbuf)
+            exchange_h(hbuf.at[me_y], hbuf)
 
 
 def _finish(h, k, v, h_out, k_out, v_out, sem):
@@ -378,7 +397,6 @@
         vm = pl.BlockSpec(memory_space=pltpu.VMEM)
         hbm = pl.BlockSpec(memory_space=pl.ANY)
         far = pl.BlockSpec(memory_space=pltpu.HBM)
-        N = X * Y
         dma = pltpu.SemaphoreType.DMA
         V = pltpu.VMEM
         scratch = [
@@ -386,7 +404,7 @@
             V((L, B, S, D), BF16), V((L, B, S, D), BF16), V((B, D, S), BF16),
             V((B + 8, BLK), BF16), V((Y, B + 8, BLK), BF16), V((Y, B, BLK), BF16),
             V((1, B), jnp.int32), V((1, D), F32),
-            V((L, 1, D), F32), V((L, N - Y, 1, D), F32), V((B, Y * BLK), BF16),
+            V((L, 1, D), F32), V((L, X - 1, 1, D), F32), V((B, Y * BLK), BF16),
             V((B, D), F32), V((B, D), F32), V((B, D), F32),
             V((L, X, B, D), BF16), V((L, X, B, D), BF16), V((L, X, B, D), BF16),
             V((L, X - 1, B, D), BF16), V((L, X - 1, B, D), BF16), V((L, 2, B, D), BF16),
@@ -395,13 +413,13 @@
             V((L, 2, B, 2 * CW), BF16), V((L, 2, B, 2 * CW), BF16), V((2, B, 2 * CW), F32),
             V((L, 4, B, CW), BF16), V((L, 4, B, CW), BF16), V((L, 8, B, CW), BF16),
             V((B, Y * BLK), F32), V((L, Y, B, BLK), BF16), V((L, Y - 1, B, BLK), BF16),
-            dma, dma((5,)), dma, dma, dma, dma((4,)), dma((2,)), dma((NC,)), dma((NC,)), dma, dma, dma,
+            dma, dma((5,)), dma, dma, dma((2,)), dma((4,)), dma((2,)), dma((L, NC)), dma((NC,)), dma, dma, dma,
         ]
         shapes = (jax.ShapeDtypeStruct((B, BLK), BF16),
                   jax.ShapeDtypeStruct((L, B, D), BF16),
                   jax.ShapeDtypeStruct((L, B, D), BF16))
         outs = pl.pallas_call(
-            functools.partial(_kernel, X, Y, float(BLK * N)),
+            functools.partial(_kernel, X, Y),
             out_shape=tuple(V(t.shape, t.dtype) for t in shapes),
             in_specs=[hbm] * 12,
             out_specs=(vm, vm, vm),

time: 46.1 us -> 44.1 us (0.957)
  Pallas kernels: 45.3 us -> 43.2 us
    pallas_call x1, Pallas kernels: 44.6 us -> 42.5 us  [body(): pl.pallas_call(functools.partial(_kernel, X, Y), out_shape=tuple((V(t.sha...]
where the time goes in v5:
time: 44.1 us; the launch traced here: 43.8 us
  Pallas kernels  43.2 us (98%)
  between operations  0.64 us (1%)
    pallas_call x1, Pallas kernels, body(): pl.pallas_call(functools.partial(_kernel, X, Y), out_shape=tuple((V(t.sha...  42.5 us

profile of v5, /device:TPU:0, one launch (start us, length us, event | category | flops | bytes accessed | tf_op | source)
XLA Modules:
  0.0 43.8 jit_solution(4731248730918733643)
XLA Ops:
  0.6 42.5 %decode_step.1 = (bf16[64,128]{1,0:T(8,128)(2,1)S(1)}, bf16[2,64,128]{2,1,0:T(8,128)(2,1)S(1)}, bf16[2,64,128]{2,1,0:T(8,128)(2,1)S(1)}) custom-call(bf16[64,128]{1,0:T(8,128)(2,1)} %h_ref.1, bf16[2,128]{1,0:T(2,128)(2,1)} %g_ref.1, s32[1,64]{1,0:T(1,128)} %bitcast.11, f32[1,128]{1,0:T(1,128)} %constant.2.clone.inv_ref, bf16[2,1024,512]{2,1,0:T(8,128)(2,1)} %wq.1, ...), custom_call_target="tpu_custom_call" | custom-call | tf_op jit(solution)/shard_map/decode_step/pallas_call | solution.py:421
  43.2 0.7 %finish.1 = (bf16[64,128]{1,0:T(8,128)(2,1)}, bf16[2,64,128]{2,1,0:T(8,128)(2,1)}, bf16[2,64,128]{2,1,0:T(8,128)(2,1)}) custom-call(bf16[64,128]{1,0:T(8,128)(2,1)S(1)} %get-tuple-element.9.h, bf16[2,64,128]{2,1,0:T(8,128)(2,1)S(1)} %get-tuple-element.10.k, bf16[2,64,128]{2,1,0:T(8,128)(2,1)S(1)} %get-tuple-element.11.v), custom_call_target="tpu_custom_call" | custom-call | tf_op jit(solution)/shard_map/finish/pallas_call | solution.py:431

commit v6 on v5

--- a/solution.py
+++ b/solution.py
@@ -54,7 +54,8 @@
     core = lax.rem(me_x, 2)
     py = [_partner(me_y, m) for m in range(Y)]
     px = [_partner(me_x, m) for m in range(X)]
-    sib, cross = px[1], px[2]
+    sib, mate = px[1], px[3]
+    part_of_f = lax.rem(core + lax.div(me_x, 2), 2)
     masks = list(range(Y - 1, 0, -1))
     near = lax.div(me_y, Y // 2)
     total = [0]
@@ -190,7 +191,7 @@
         for m in (2, 3, 1):
             remote(pq.at[l, px[m]], rq.at[l, m - 1], qrecv.at[0], me_y, px[m])
         part(1, pk)
-        for i, t in enumerate((px[3], sib)):
+        for i, t in enumerate((px[2], sib)):
             remote(pk.at[l, t], rks.at[l, i], qrecv.at[1], me_y, sib)
         part(2, pv)
         for m in (2, 3, 1):
@@ -202,7 +203,7 @@
             return jnp.dot(xs[...], win_b[l, :, cols], preferred_element_type=F32)
 
         def f_sib(i):
-            fsib[l, i] = f_part(1 - core, i).astype(BF16)
+            fsib[l, i] = f_part(1 - part_of_f, i).astype(BF16)
             remote(fsib.at[l, i], fsibr.at[l, i], arecv.at[i], me_y, sib)
 
         def f_add(i):
@@ -214,10 +215,10 @@
             for c, (q0, nq) in enumerate(QUARTERS):
                 if q0 // 2 == i:
                     qs = pl.ds(q0, nq)
-                    remote(fcross.at[l, qs], fcrossr.at[l, qs], brecv.at[l, c], me_y, cross)
+                    remote(fcross.at[l, qs], fcrossr.at[l, qs], brecv.at[l, c], me_y, mate)
 
         f_sib(0)
-        fown[0] = f_part(core, 0)
+        fown[0] = f_part(part_of_f, 0)
         wait_bytes(mrow.at[l, 0], mrecv.at[0], "w_ms")
         ss1, G1 = column(mrow[l, 0]), mrow[l, 0, :, B:B + 1]
         ssc, Gc = ss + ss1, jnp.maximum(G, G1)
@@ -225,11 +226,11 @@
         w_own = sc_ * rms(ss, NX) * (G / Gc)
         w_sib = sc_ * rms(ss1, NX) * (G1 / Gc)
         wait_bytes(rks.at[l], qrecv.at[1], "w_ks")
-        kx[l] = (pk[l, cross].astype(F32) * w_own + rks[l, 0].astype(F32) * w_sib).astype(BF16)
-        remote(kx.at[l], rkx.at[l], qrecv.at[3], me_y, cross)
+        kx[l] = (pk[l, mate].astype(F32) * w_own + rks[l, 0].astype(F32) * w_sib).astype(BF16)
+        remote(kx.at[l], rkx.at[l], qrecv.at[3], me_y, mate)
         f_sib(1)
         f_add(0)
-        fown[1] = f_part(core, 1)
+        fown[1] = f_part(part_of_f, 1)
         f_add(1)
 
         scale = D ** -0.5
@@ -278,8 +279,10 @@
         def values(i, p):
             b0 = i * GB
             acc = jnp.zeros((GB, D), F32)
-            for j in range(GB):
-                acc = jnp.where(orow == j, jnp.dot(p, v_b[l, b0 + j], preferred_element_type=F32), acc)
+            for j in range(0, GB, 2):
+                pair = jnp.concatenate([v_b[l, b0 + j], v_b[l, b0 + j + 1]], axis=1)
+                t = jnp.dot(p, pair, preferred_element_type=F32)
+                acc = jnp.where(orow == j, t[:, :D], jnp.where(orow == j + 1, t[:, D:], acc))
             of32[b0:b0 + GB, :] = acc
 
         with jax.named_scope("attn"):
@@ -288,10 +291,10 @@
                 cur = scores(i)
                 values(i - 1, prev)
                 prev = cur
-            values(B // GB - 1, prev)
 
         wait_bytes(rv.at[l], qrecv.at[2], "w_nv")
         wait_bytes(rkx.at[l], qrecv.at[3], "w_nk")
+        values(B // GB - 1, prev)
         v = joined(pv[l, me_x], rv[l])
         k = rope(chips(pk[l, me_x].astype(F32) * w_own + rks[l, 1].astype(F32) * w_sib, rkx[l].astype(F32)))
         sn = jnp.sum(q_b[...].astype(F32) * k.astype(F32), axis=1, keepdims=True) * scale
@@ -311,7 +314,7 @@
             rows = pl.ds(pl.multiple_of(q0 * CW, CW), nq * CW)
             return jnp.dot(f, wout_b[l, rows, cols], preferred_element_type=F32)
 
-        mine, other = core * 4, (1 - core) * 4
+        mine, other = part_of_f * 4, (1 - part_of_f) * 4
         everything = slice(None)
         for c, (q0, nq) in enumerate(QUARTERS):
             wait_bytes(fcrossr.at[l, pl.ds(q0, nq)], brecv.at[l, c], "w_fc")
@@ -330,10 +333,10 @@
                 yacc[...] = yacc[...] + (f_dot(mine + q0, nq, everything) + f_dot(other + p0, np_, everything))
         p0, np_ = QUARTERS[1]
         wait_bytes(fbuf.at[l, pl.ds(p0, np_)], crecv.at[1], "w_fg")
+        yacc[...] = yacc[...] + f_dot(other + p0, np_, everything)
         wait_bytes(obuf.at[l, pl.ds(0, X - 1)], orecv, "w_og")
         og = jnp.concatenate([obuf[l, j] for j in range(X)], axis=1)
-        yacc[...] = yacc[...] + (f_dot(other + p0, np_, everything)
-                                 + jnp.dot(og, wo_b[l], preferred_element_type=F32))
+        yacc[...] = yacc[...] + jnp.dot(og, wo_b[l], preferred_element_type=F32)
         p0, np_ = QUARTERS[2]
         wait_bytes(fbuf.at[l, pl.ds(p0, np_)], crecv.at[2], "w_fg")
         W = Y // 2 * BLK

time: 44.1 us -> 43.5 us (0.986)
  Pallas kernels: 43.2 us -> 42.6 us
    pallas_call x1, Pallas kernels: 42.5 us -> 41.9 us  [body(): pl.pallas_call(functools.partial(_kernel, X, Y), out_shape=tuple((V(t.sha...]
where the time goes in v6:
time: 43.5 us; the launch traced here: 43.2 us
  Pallas kernels  42.6 us (98%)
  between operations  0.64 us (1%)
    pallas_call x1, Pallas kernels, body(): pl.pallas_call(functools.partial(_kernel, X, Y), out_shape=tuple((V(t.sha...  41.9 us

profile of v6, /device:TPU:0, one launch (start us, length us, event | category | flops | bytes accessed | tf_op | source)
XLA Modules:
  0.0 43.2 jit_solution(16319643238226402682)
XLA Ops:
  0.6 41.9 %decode_step.1 = (bf16[64,128]{1,0:T(8,128)(2,1)S(1)}, bf16[2,64,128]{2,1,0:T(8,128)(2,1)S(1)}, bf16[2,64,128]{2,1,0:T(8,128)(2,1)S(1)}) custom-call(bf16[64,128]{1,0:T(8,128)(2,1)} %h_ref.1, bf16[2,128]{1,0:T(2,128)(2,1)} %g_ref.1, s32[1,64]{1,0:T(1,128)} %bitcast.11, f32[1,128]{1,0:T(1,128)} %constant.2.clone.inv_ref, bf16[2,1024,512]{2,1,0:T(8,128)(2,1)} %wq.1, ...), custom_call_target="tpu_custom_call" | custom-call | tf_op jit(solution)/shard_map/decode_step/pallas_call | solution.py:424
  42.6 0.7 %finish.1 = (bf16[64,128]{1,0:T(8,128)(2,1)}, bf16[2,64,128]{2,1,0:T(8,128)(2,1)}, bf16[2,64,128]{2,1,0:T(8,128)(2,1)}) custom-call(bf16[64,128]{1,0:T(8,128)(2,1)S(1)} %get-tuple-element.9.h, bf16[2,64,128]{2,1,0:T(8,128)(2,1)S(1)} %get-tuple-element.10.k, bf16[2,64,128]{2,1,0:T(8,128)(2,1)S(1)} %get-tuple-element.11.v), custom_call_target="tpu_custom_call" | custom-call | tf_op jit(solution)/shard_map/finish/pallas_call | solution.py:434

commit v7 on v6

--- a/solution.py
+++ b/solution.py
@@ -39,7 +39,7 @@
             hx, hbuf0, hbuf, lens_b, inv_b, mown, mrow, xs, cos_b, sin_b, lenb,
             pq, pk, pv, rq, rv, rks, kx, rkx, q_b, m_b, d_b, of32, obuf,
             fsib, fsibr, fown, fcross, fcrossr, fbuf, yacc, ybuf, ry,
-            isem, wsem, sent, hrecv, mrecv, qrecv, arecv, brecv, crecv, orecv, ysend, yrecv):
+            wsem, sent, hrecv, mrecv, qrecv, arecv, brecv, crecv, orecv, yrecv):
     me_y = lax.axis_index("yz")
     me_x = lax.axis_index("x")
     L = wqkv_b.shape[0]
@@ -57,7 +57,6 @@
     sib, mate = px[1], px[3]
     part_of_f = lax.rem(core + lax.div(me_x, 2), 2)
     masks = list(range(Y - 1, 0, -1))
-    near = lax.div(me_y, Y // 2)
     total = [0]
 
     barrier = pltpu.get_barrier_semaphore()
@@ -66,17 +65,15 @@
     for n in range(X - 1, 0, -1):
         pl.semaphore_signal(barrier, inc=1, device_id=(me_y, px[n]), device_id_type=MESH)
 
-    def remote(src, dst, recv, y, x, send=None):
-        if send is None:
-            total[0] += math.prod(src.shape) * np.dtype(src.dtype).itemsize
-        pltpu.make_async_remote_copy(src, dst, sent if send is None else send, recv,
-                                     device_id=(y, x), device_id_type=MESH).start()
+    def remote(src, dst, recv, y, x):
+        total[0] += math.prod(src.shape) * np.dtype(src.dtype).itemsize
+        pltpu.make_async_remote_copy(src, dst, sent, recv, device_id=(y, x), device_id_type=MESH).start()
 
     def wait_bytes(ref, sem, name="wait"):
         with jax.named_scope(name):
             pltpu.make_async_copy(ref, ref, sem).wait()
 
-    inputs = [pltpu.make_async_copy(s, d, isem) for s, d in (
+    inputs = [pltpu.make_async_copy(s, d, wsem.at[0]) for s, d in (
         (h_ref, hx.at[pl.ds(0, B)]), (g_ref, hx.at[pl.ds(B, L)]), (lens_ref, lens_b), (inv_ref, inv_b))]
     for c in inputs:
         c.start()
@@ -339,21 +336,21 @@
         yacc[...] = yacc[...] + jnp.dot(og, wo_b[l], preferred_element_type=F32)
         p0, np_ = QUARTERS[2]
         wait_bytes(fbuf.at[l, pl.ds(p0, np_)], crecv.at[2], "w_fg")
-        W = Y // 2 * BLK
-        for hz, ms in ((1 - near, masks[:Y // 2]), (near, masks[Y // 2:])):
-            cols = pl.ds(pl.multiple_of(hz * W, W), W)
+        W = 2 * BLK
+        for c in range(Y // 2):
+            z = lax.div(py[masks[2 * c]], 2)
+            cols = pl.ds(pl.multiple_of(z * W, W), W)
             acc = yacc[:, cols] + f_dot(other + p0, np_, cols)
-            for j in range(Y // 2):
-                ybuf[l, hz * (Y // 2) + j] = acc[:, j * BLK:(j + 1) * BLK].astype(BF16)
-            for m in ms:
-                remote(ybuf.at[l, py[m]], ry.at[l, m - 1], yrecv, py[m], me_x, ysend if last else None)
+            for j in range(2):
+                ybuf[l, z * 2 + j] = acc[:, j * BLK:(j + 1) * BLK].astype(BF16)
+            for m in masks[2 * c:2 * c + 2]:
+                remote(ybuf.at[l, py[m]], ry.at[l, m - 1], yrecv, py[m], me_x)
         if last:
             n = total[0]
             big = S * D * 2
             wait_bytes(k_b.at[0, pl.ds(0, n // big)], sent)
             if n % big:
                 wait_bytes(k_b.at[0, 0, pl.ds(0, n % big // (2 * D))], sent)
-            wait_bytes(ry.at[l], ysend)
         else:
             transpose_k(l + 1)
         wait_bytes(ry.at[l], yrecv, "w_y")
@@ -416,7 +413,7 @@
             V((L, 2, B, 2 * CW), BF16), V((L, 2, B, 2 * CW), BF16), V((2, B, 2 * CW), F32),
             V((L, 4, B, CW), BF16), V((L, 4, B, CW), BF16), V((L, 8, B, CW), BF16),
             V((B, Y * BLK), F32), V((L, Y, B, BLK), BF16), V((L, Y - 1, B, BLK), BF16),
-            dma, dma((5,)), dma, dma, dma((2,)), dma((4,)), dma((2,)), dma((L, NC)), dma((NC,)), dma, dma, dma,
+            dma((5,)), dma, dma, dma((2,)), dma((4,)), dma((2,)), dma((L, NC)), dma((NC,)), dma, dma,
         ]
         shapes = (jax.ShapeDtypeStruct((B, BLK), BF16),
                   jax.ShapeDtypeStruct((L, B, D), BF16),

time: 43.5 us -> 43.4 us (level)
  no operation moved by 1% of the time
where the time goes in v7:
time: 43.4 us; the launch traced here: 43.2 us
  Pallas kernels  42.5 us (98%)
  between operations  0.64 us (1%)
    pallas_call x1, Pallas kernels, body(): pl.pallas_call(functools.partial(_kernel, X, Y), out_shape=tuple((V(t.sha...  41.9 us

profile of v7, /device:TPU:0, one launch (start us, length us, event | category | flops | bytes accessed | tf_op | source)
XLA Modules:
  0.0 43.2 jit_solution(14854314439502391736)
XLA Ops:
  0.6 41.9 %decode_step.1 = (bf16[64,128]{1,0:T(8,128)(2,1)S(1)}, bf16[2,64,128]{2,1,0:T(8,128)(2,1)S(1)}, bf16[2,64,128]{2,1,0:T(8,128)(2,1)S(1)}) custom-call(bf16[64,128]{1,0:T(8,128)(2,1)} %h_ref.1, bf16[2,128]{1,0:T(2,128)(2,1)} %g_ref.1, s32[1,64]{1,0:T(1,128)} %bitcast.11, f32[1,128]{1,0:T(1,128)} %constant.2.clone.inv_ref, bf16[2,1024,512]{2,1,0:T(8,128)(2,1)} %wq.1, ...), custom_call_target="tpu_custom_call" | custom-call | tf_op jit(solution)/shard_map/decode_step/pallas_call | solution.py:421
  42.5 0.7 %finish.1 = (bf16[64,128]{1,0:T(8,128)(2,1)}, bf16[2,64,128]{2,1,0:T(8,128)(2,1)}, bf16[2,64,128]{2,1,0:T(8,128)(2,1)}) custom-call(bf16[64,128]{1,0:T(8,128)(2,1)S(1)} %get-tuple-element.9.h, bf16[2,64,128]{2,1,0:T(8,128)(2,1)S(1)} %get-tuple-element.10.k, bf16[2,64,128]{2,1,0:T(8,128)(2,1)S(1)} %get-tuple-element.11.v), custom_call_target="tpu_custom_call" | custom-call | tf_op jit(solution)/shard_map/finish/pallas_call | solution.py:431
